TPU v7x, 32 devices: a whole 2x2x4 slice. The times are simulated.
32 devices in a mesh: rep: 4 (over y, core), grp: 8 (over z, x).
Axes of the slice: x: 2, y: 2, z: 4, core: 2. Of those that a mesh axis runs over, the one named last changes fastest.
Arguments:
- hidden_in: bfloat16 [128, 7168], P(('rep', 'grp')), may hold values from -3 to 3
- q_nope: bfloat16 [128, 8192], P(('rep', 'grp')), may hold values from -9 to 9
- q_rope: bfloat16 [128, 4096], P(('rep', 'grp')), may hold values from -36 to 36
- new_kv: bfloat16 [128, 576], P(('rep', 'grp')), may hold values from -6 to 6
- cache_kv: bfloat16 [128, 4096, 576], P(('rep', 'grp')), may hold values from -10 to 10
- lengths: int32 [128], P(('rep', 'grp')), may hold values from 2 to 4096, as said below
- w_uk: bfloat16 [512, 8192], P('rep'), may hold values from -0.5 to 0.5
- w_uv: bfloat16 [512, 8192], P('rep'), may hold values from -0.25 to 0.25
- w_out: bfloat16 [8192, 7168], P('grp'), may hold values from -0.0625 to 0.0625
- norm_gain: bfloat16 [7168], replicated, may hold values from 0.5 to 1.5
- w_gate: bfloat16 [7168, 18432], P(None, ('rep', 'grp')), may hold values from -0.0625 to 0.0625
- w_up: bfloat16 [7168, 18432], P(None, ('rep', 'grp')), may hold values from -0.0625 to 0.0625
- w_down: bfloat16 [18432, 7168], P(('rep', 'grp')), may hold values from -0.046875 to 0.046875
Outputs:
- hidden_out: bfloat16 [128, 7168], P(('rep', 'grp'))
Inputs may be any that keep to these rules, and one draw needn't show every extreme that they name: `lengths`: every sequence has 2 or more cached positions and at most 4096; some sequence has exactly 4096.
All inputs are finite; a program needn't handle non-finite values.
Results may differ from a plain program's by a relative error of at most 0.03.
Values may be sent and summed in bfloat16 or wider, within the bound.
A program may use at most 192 MiB of HBM per device.

v0:
```python
import jax
import jax.numpy as jnp
from jax import lax
from jax.sharding import PartitionSpec as P

H = 64
NOPE = 128
ROPE = 64
VH = 128
KV_RANK = 512
CACHE = 4096


epsilon = 1e-06


def norm_rows(resid, norm_gain):
    resid_f32 = resid.astype(jnp.float32)
    mean_sq = jnp.mean(resid_f32 * resid_f32, axis=1, keepdims=True)
    return (resid_f32 * lax.rsqrt(mean_sq + epsilon) * norm_gain.astype(jnp.float32)).astype(
        jnp.bfloat16
    )


def gated_rows(rows_in, gate_cols, up_cols):
    gate_val = jnp.dot(rows_in, gate_cols, preferred_element_type=jnp.float32)
    up_val = jnp.dot(rows_in, up_cols, preferred_element_type=jnp.float32)
    return (jax.nn.silu(gate_val) * up_val).astype(jnp.bfloat16)


def on_device(
    hidden_in,
    q_nope,
    q_rope,
    new_kv,
    cache_kv,
    lengths,
    w_uk,
    w_uv,
    w_out,
    norm_gain,
    w_gate,
    w_up,
    w_down,
):
    seq_count = hidden_in.shape[0]
    key_up, value_up = (
        lax.all_gather(w_uk, "rep", axis=0, tiled=True),
        lax.all_gather(w_uv, "rep", axis=0, tiled=True),
    )
    nope_part = q_nope.reshape(seq_count, H, NOPE)
    q_lat = jnp.einsum(
        "bhd,chd->bhc",
        nope_part,
        key_up.reshape(KV_RANK, H, NOPE),
        preferred_element_type=jnp.float32,
    ).astype(jnp.bfloat16)
    queries = jnp.concatenate([q_lat, q_rope.reshape(seq_count, H, ROPE)], axis=2)
    score_scale = float(NOPE + ROPE) ** (-0.5)
    scores = (
        jnp.einsum("bhc,blc->bhl", queries, cache_kv, preferred_element_type=jnp.float32)
        * score_scale
    )
    positions = lax.broadcasted_iota(jnp.int32, (1, 1, CACHE), 2)
    scores = jnp.where(positions < lengths[:, None, None], scores, -jnp.inf)
    own_score = (
        jnp.einsum("bhc,bc->bh", queries, new_kv, preferred_element_type=jnp.float32) * score_scale
    )
    row_top = jnp.maximum(jnp.max(scores, axis=2), own_score)
    weights = jnp.exp(scores - row_top[:, :, None])
    own_weight = jnp.exp(own_score - row_top)
    denom_sum = jnp.sum(weights, axis=2) + own_weight
    softmax_w = (weights / denom_sum[:, :, None]).astype(jnp.bfloat16)
    own_prob = (own_weight / denom_sum).astype(jnp.bfloat16)
    mixture = jnp.einsum("bhl,blc->bhc", softmax_w, cache_kv, preferred_element_type=jnp.float32)
    mixture = (
        mixture + own_prob.astype(jnp.float32)[:, :, None] * new_kv.astype(jnp.float32)[:, None, :]
    )
    latent = mixture[:, :, :KV_RANK].astype(jnp.bfloat16)
    head_out = jnp.einsum(
        "bhc,che->bhe", latent, value_up.reshape(KV_RANK, H, VH), preferred_element_type=jnp.float32
    ).astype(jnp.bfloat16)
    regrouped = lax.all_to_all(head_out, "grp", split_axis=1, concat_axis=0, tiled=True)
    group_count = regrouped.shape[0]
    partial_value = jnp.dot(
        regrouped.reshape(group_count, -1), w_out, preferred_element_type=jnp.float32
    )
    offset = lax.axis_index("grp") * seq_count
    own_part = lax.dynamic_slice_in_dim(partial_value, offset, seq_count, 0) + hidden_in.astype(
        jnp.float32
    )
    partial_value = lax.dynamic_update_slice_in_dim(partial_value, own_part, offset, 0)
    summed = lax.psum(partial_value.astype(jnp.bfloat16), "grp")
    normed_group = norm_rows(summed, norm_gain)
    resid_own = lax.dynamic_slice_in_dim(summed, offset, seq_count, 0)
    every_row = lax.all_gather(normed_group, "rep", axis=0, tiled=True)
    activated = gated_rows(every_row, w_gate, w_up)
    mlp_out = lax.psum_scatter(
        jnp.dot(activated, w_down, preferred_element_type=jnp.float32),
        ("rep", "grp"),
        scatter_dimension=0,
        tiled=True,
    )
    return (resid_own.astype(jnp.float32) + mlp_out).astype(jnp.bfloat16)


def solution(mesh):
    return jax.shard_map(
        on_device,
        mesh=mesh,
        in_specs=(
            P(("rep", "grp"), None),
            P(("rep", "grp"), None),
            P(("rep", "grp"), None),
            P(("rep", "grp"), None),
            P(("rep", "grp"), None, None),
            P(("rep", "grp")),
            P("rep", None),
            P("rep", None),
            P("grp", None),
            P(),
            P(None, ("rep", "grp")),
            P(None, ("rep", "grp")),
            P(("rep", "grp"), None),
        ),
        out_specs=P(("rep", "grp"), None),
        check_vma=False,
    )
```

profile of v0, /device:TPU:0, one launch (start us, length us, event | category | flops | bytes accessed | tf_op | source)
XLA Modules:
  0.0 423.2 jit_solution(15201797613449492282)
XLA Ops:
  6.5 0.0 copy-start
  6.5 0.0 copy-start.3
  6.5 0.0 all-gather.4.cloned.1.call-start
  6.5 4.2 copy.26
  10.8 0.0 copy-start.5
  10.8 0.0 copy-start.7
  10.8 0.0 copy-start.8
  10.8 0.0 all-gather.4.cloned.1.call-update
  10.8 0.0 all-gather.6.cloned.1.call-start
  10.8 0.0 copy-done.3
  10.8 2.4 copy.31
  13.3 0.0 all-gather.6.cloned.1.call-update
  13.3 0.0 copy-done.5
  13.3 0.1 reshape.52
  13.4 0.1 copy.29
  13.5 0.0 copy-done.7
  13.5 0.0 copy-done.8
  13.5 0.1 iota_compare_fusion
  13.6 59.4 %all-gather.4.cloned.1.call-done = bf16[512,8192]{0,1:T(8,128)(2,1)} async-done(((bf16[128,8192]{0,1:T(8,128)(2,1)}), bf16[512,8192]{0,1:T(8,128)(2,1)}) %all-gather.4.cloned.1.call-update) | async-done | bytes 8388624 | tf_op jit(solution)/shard_map/all_gather | solution.py:48
  73.0 0.0 copy-done
  73.1 4.6 %fusion.5 = bf16[4,64,512]{2,0,1:T(4,128)(2,1)S(1)} fusion(bf16[512,64,128]{0,2,1:T(8,128)(2,1)} %bitcast.30, bf16[4,8192]{1,0:T(4,128)(2,1)S(1)} %copy-done), kind=kOutput, calls=%fused_computation.10 | convolution fusion | flops 33685504 | bytes 8716288 | tf_op jit(solution)/shard_map/bhd,chd->bhc/dot_general | solution.py:52
  77.6 0.2 pad_maximum_fusion
  77.8 0.2 fusion.18
  78.0 10.5 %fusion.32 = (f32[4,64]{1,0:T(4,128)S(1)}, f32[4,64,4096]{2,1,0:T(8,128)S(1)}) fusion(bf16[4,4096,576]{1,2,0:T(8,128)(2,1)} %param.17, bf16[4,64,576]{2,0,1:T(4,128)(2,1)S(1)} %pad_maximum_fusion, pred[4,4096]{1,0:T(4,128)(4,1)S(1)} %iota_compare_fusion), kind=kOutput, calls=%fused_computation.49 | convolution fusion | flops 1211105024 | bytes 23380992 | tf_op jit(solution)/shard_map/bhc,blc->bhl/dot_general | solution.py:61
  88.5 0.7 fusion.1
  89.2 9.8 %fusion.2 = f32[4,64,576]{2,1,0:T(8,128)S(1)} fusion(bf16[4,4096,576]{1,2,0:T(8,128)(2,1)} %param.17, f32[4,64,4096]{2,1,0:T(8,128)S(1)} %get-tuple-element.8, f32[4,64]{1,0:T(4,128)S(1)} %get-tuple-element.6, f32[4,64]{1,0:T(4,128)S(1)} %multiply_maximum_fusion), kind=kOutput, calls=%fused_computation.5 | convolution fusion | flops 1211105280 | bytes 23660544 | tf_op jit(solution)/shard_map/bhl,blc->bhc/dot_general | solution.py:75
  99.0 0.1 fusion.12
  99.1 34.9 %all-gather.6.cloned.1.call-done = bf16[512,8192]{0,1:T(8,128)(2,1)} async-done(((bf16[128,8192]{0,1:T(8,128)(2,1)}), bf16[512,8192]{0,1:T(8,128)(2,1)}) %all-gather.6.cloned.1.call-update) | async-done | bytes 8388624 | tf_op jit(solution)/shard_map/all_gather | solution.py:49
  134.0 6.3 %fusion.7 = bf16[4,64,128]{2,0,1:T(4,128)(2,1)} fusion(bf16[512,64,128]{0,2,1:T(8,128)(2,1)} %bitcast.29, bf16[4,64,512]{2,1,0:T(8,128)(2,1)S(1)} %fusion.12), kind=kOutput, calls=%fused_computation.15 | convolution fusion | flops 33587200 | bytes 8716288 | tf_op jit(solution)/shard_map/bhc,che->bhe/dot_general | solution.py:80
  140.3 5.5 %all-to-all-start = ((bf16[4,64,128]{2,0,1:T(4,128)(2,1)}), bf16[4,64,128]{2,0,1:T(4,128)(2,1)S(1)}, u32[]{:S(2)}, u32[]{:S(2)}) async-start(bf16[4,64,128]{2,0,1:T(4,128)(2,1)} %fusion.7), calls=%async_computation | async-start | bytes 131072 | tf_op jit(solution)/shard_map/all_to_all | solution.py:83
  145.8 0.0 all-reduce.4.cloned.1.call-start
  145.9 6.9 %all-to-all-done = bf16[4,64,128]{2,0,1:T(4,128)(2,1)S(1)} async-done(((bf16[4,64,128]{2,0,1:T(4,128)(2,1)}), bf16[4,64,128]{2,0,1:T(4,128)(2,1)S(1)}, u32[]{:S(2)}, u32[]{:S(2)}) %all-to-all-start) | async-done | bytes 65568 | tf_op jit(solution)/shard_map/all_to_all | solution.py:83
  152.7 0.0 copy-start.4
  152.7 0.0 copy-start.6
  152.7 7.8 %fusion.24 = f32[32,7168]{1,0:T(8,128)S(1)} fusion(bf16[1024,7168]{1,0:T(8,128)(2,1)} %param.21, bf16[4,8,8,128]{3,2,1,0:T(8,128)(2,1)S(1)} %bitcast.31), kind=kOutput, calls=%fused_computation.36 | convolution fusion | flops 469762048 | bytes 15663104 | tf_op jit(solution)/shard_map/dot_general | solution.py:85
  160.6 0.0 copy-done.4
  160.6 0.1 add_dynamic-update-slice_fusion
  160.6 0.8 convert_element_type.58
  161.5 0.0 all-reduce.4.cloned.1.call-update
  161.5 0.0 all-gather.8.cloned.1.call-start
  161.5 0.0 copy-done.6
  161.6 69.0 %all-reduce.4.cloned.1.call-done = bf16[32,7168]{1,0:T(8,128)(2,1)} async-done(((bf16[32,7168]{1,0:T(8,128)(2,1)}), bf16[32,7168]{1,0:T(8,128)(2,1)}) %all-reduce.4.cloned.1.call-update) | async-done | bytes 458768 | tf_op jit(solution)/shard_map/psum | solution.py:93
  230.5 1.2 fusion.8
  231.8 2.0 fusion.10
  233.7 0.0 all-gather.8.cloned.1.call-update
  233.8 0.2 all-reduce.6.cloned.1.call-start
  234.0 20.3 %all-gather.8.cloned.1.call-done = bf16[128,7168]{1,0:T(8,128)(2,1)} async-done(((bf16[32,7168]{1,0:T(8,128)(2,1)}), bf16[128,7168]{1,0:T(8,128)(2,1)}) %all-gather.8.cloned.1.call-update) | async-done | bytes 1835024 | tf_op jit(solution)/shard_map/all_gather | solution.py:96
  254.3 0.0 copy-start.2
  254.3 6.3 %fusion.33 = f32[128,576]{0,1:T(8,128)S(1)} fusion(bf16[128,7168]{1,0:T(8,128)(2,1)} %all-gather.8.cloned.1.call-done, bf16[7168,576]{0,1:T(8,128)(2,1)} %param.23), kind=kOutput, calls=%fused_computation.50 | convolution fusion | flops 1056964608 | bytes 10387456 | tf_op jit(solution)/shard_map/dot_general | solution.py:26
  260.6 0.0 copy-done.2
  260.6 0.0 copy-start.1
  260.7 14.2 %fusion.11 = f32[128,7168]{1,0:T(8,128)} fusion(bf16[576,7168]{1,0:T(8,128)(2,1)} %param.25, bf16[128,7168]{1,0:T(8,128)(2,1)S(1)} %copy-done.2, bf16[7168,576]{0,1:T(8,128)(2,1)} %param.24, f32[128,576]{0,1:T(8,128)S(1)} %fusion.33), kind=kOutput, calls=%fused_computation.19 | convolution fusion | flops 2114371584 | bytes 22315008 | tf_op jit(solution)/shard_map/dot_general | solution.py:99
  274.9 0.0 all-reduce.6.cloned.1.call-update
  274.9 140.1 %all-reduce.6.cloned.1.call-done = f32[128,7168]{1,0:T(8,128)} async-done(((f32[128,7168]{1,0:T(8,128)}), f32[128,7168]{1,0:T(8,128)}) %all-reduce.6.cloned.1.call-update) | async-done | bytes 3670032
  415.0 1.7 fusion.23
  416.7 0.0 copy-done.1
  (6 shorter events, 0.0 us)
Async XLA Ops:
  6.5 66.5 %copy-start = (bf16[4,8192]{1,0:T(4,128)(2,1)S(1)}, bf16[4,8192]{1,0:T(4,128)(2,1)}, u32[]{:S(2)}) copy-start(bf16[4,8192]{1,0:T(4,128)(2,1)} %param.14) | copy-start | bytes 196612
  6.5 4.3 %copy-start.3 = (bf16[128,8192]{1,0:T(8,128)(2,1)S(1)}, bf16[128,8192]{1,0:T(8,128)(2,1)}, u32[]{:S(2)}) copy-start(bf16[128,8192]{1,0:T(8,128)(2,1)} %param.20) | copy-start | bytes 6291460
  6.5 66.5 %all-gather.4.cloned.1.call-start = ((), (), s32[]{:S(2)}) async-start(), calls=%async_computation.1 | async-start | bytes 10485760 | tf_op jit(solution)/shard_map/all_gather | solution.py:48
  10.8 2.6 copy-start.5
  10.8 2.8 copy-start.7
  10.8 2.8 copy-start.8
  10.8 123.2 %all-gather.6.cloned.1.call-start = ((), (), s32[]{:S(2)}) async-start(), calls=%async_computation.2 | async-start | bytes 10485760 | tf_op jit(solution)/shard_map/all_gather | solution.py:49
  140.3 12.4 %all-to-all-start = ((bf16[4,64,128]{2,0,1:T(4,128)(2,1)}), bf16[4,64,128]{2,0,1:T(4,128)(2,1)S(1)}, u32[]{:S(2)}, u32[]{:S(2)}) async-start(bf16[4,64,128]{2,0,1:T(4,128)(2,1)} %fusion.7), calls=%async_computation | async-start | bytes 131072 | tf_op jit(solution)/shard_map/all_to_all | solution.py:83
  145.8 84.7 %all-reduce.4.cloned.1.call-start = ((), (), s32[]{:S(2)}) async-start(), calls=%async_computation.3 | async-start | bytes 917504 | tf_op jit(solution)/shard_map/psum | solution.py:93
  152.7 7.8 %copy-start.4 = (bf16[4,7168]{1,0:T(4,128)(2,1)S(1)}, bf16[4,7168]{1,0:T(4,128)(2,1)}, u32[]{:S(2)}) copy-start(bf16[4,7168]{1,0:T(4,128)(2,1)} %param.13) | copy-start | bytes 172036
  152.7 8.8 %copy-start.6 = (bf16[7168]{0:T(1024)(128)(2,1)S(1)}, bf16[7168]{0:T(1024)(128)(2,1)}, u32[]{:S(2)}) copy-start(bf16[7168]{0:T(1024)(128)(2,1)} %param.22) | copy-start | bytes 43012
  161.5 92.8 %all-gather.8.cloned.1.call-start = ((), (), s32[]{:S(2)}) async-start(), calls=%async_computation.4 | async-start | bytes 2293760 | tf_op jit(solution)/shard_map/all_gather | solution.py:96
  233.8 181.2 %all-reduce.6.cloned.1.call-start = ((), (), s32[]{:S(2)}) async-start(), calls=%async_computation.5 | async-start | bytes 7340032
  254.3 6.3 %copy-start.2 = (bf16[128,7168]{1,0:T(8,128)(2,1)S(1)}, bf16[128,7168]{1,0:T(8,128)(2,1)}, u32[]{:S(2)}) copy-start(bf16[128,7168]{1,0:T(8,128)(2,1)} %all-gather.8.cloned.1.call-done) | copy-start | bytes 5505028
  260.6 156.0 %copy-start.1 = (bf16[4,8192]{1,0:T(4,128)(2,1)S(1)}, bf16[4,8192]{1,0:T(4,128)(2,1)}, u32[]{:S(2)}) copy-start(bf16[4,8192]{1,0:T(4,128)(2,1)} %param.14) | copy-start | bytes 196612
Sparse Core Ops, SparseCore 0:
  10.9 62.0 all-gather.3
  74.6 59.3 all-gather.5
  161.6 68.8 all-reduce.3
  233.9 20.3 all-gather.7
  275.0 139.9 all-reduce.5
where the time goes:
time: 424 us; the launch traced here: 423 us
  waiting for transfers between devices  331 us (78%)
  matrix products  59.6 us (14%)
  between operations  13.3 us (3%)
  local copies, waits for them, and re-layouts  6.89 us (2%)
  other arithmetic  6.88 us (2%)
  starting transfers between devices  5.86 us (1%)
    unnamed x6, waiting for transfers between devices  140 us
    psum x1, waiting for transfers between devices, on_device(): summed = lax.psum(partial_value.astype(jnp.bfloat16), 'grp')  69 us
    all_gather x1, waiting for transfers between devices, on_device(): lax.all_gather(w_uk, 'rep', axis=0, tiled=True)  59.4 us
    all_gather x1, waiting for transfers between devices, on_device(): lax.all_gather(w_uv, 'rep', axis=0, tiled=True)  34.9 us
    all_gather x1, waiting for transfers between devices, on_device(): every_row = lax.all_gather(normed_group, 'rep', axis=0, tiled=True)  20.3 us
    dot_general x1, matrix products, on_device(): jnp.dot(activated, w_down, preferred_element_type=jnp.float32)  14.2 us
    dot_general x1, matrix products, on_device(): jnp.einsum('bhc,blc->bhl', queries, cache_kv, preferred_element_type=jnp....  10.5 us
    dot_general x1, matrix products, on_device(): jnp.einsum('bhl,blc->bhc', softmax_w, cache_kv, preferred_element_type=jn...  9.77 us
  transfers between devices with their start and end apart: 6, of which 6 were waited for; matrix products, arithmetic and copies ran while one was open for 7% of the time, Pallas kernels for 0%

commit v1 on v0

v1 whole, which is shorter than its diff:
```python
import functools

import jax
import jax.numpy as jnp
from jax import lax
from jax.experimental import pallas as pl
from jax.experimental.pallas import tpu as pltpu
from jax.sharding import PartitionSpec as P

H = 64
NOPE = 128
ROPE = 64
VH = 128
KV_RANK = 512
CACHE = 4096
MESH = pl.DeviceIdType.MESH

epsilon = 1e-06


def _exchange_kernel(axis, n, gather, x_ref, out_ref, send_sem, recv_sem, own_sem):
    me = lax.axis_index(axis)
    barrier = pltpu.get_barrier_semaphore()

    def greet(k, carry):
        peer = lax.rem(me + k, n)
        pl.semaphore_signal(barrier, inc=1, device_id={axis: peer}, device_id_type=MESH)
        return carry

    lax.fori_loop(1, n, greet, 0)
    own = pltpu.make_async_copy(x_ref if gather else x_ref.at[me], out_ref.at[me], own_sem)
    own.start()
    pl.semaphore_wait(barrier, n - 1)

    def send(k, carry):
        peer = lax.rem(me + k, n)
        pltpu.make_async_remote_copy(
            src_ref=x_ref if gather else x_ref.at[peer],
            dst_ref=out_ref.at[me],
            send_sem=send_sem.at[k - 1],
            recv_sem=recv_sem.at[k - 1],
            device_id={axis: peer},
            device_id_type=MESH,
        ).start()
        return carry

    lax.fori_loop(1, n, send, 0)
    own.wait()

    def finish(k, carry):
        source = lax.rem(me + n - k, n)
        peer = lax.rem(me + k, n)
        pltpu.make_async_remote_copy(
            src_ref=x_ref if gather else x_ref.at[peer],
            dst_ref=out_ref.at[source],
            send_sem=send_sem.at[k - 1],
            recv_sem=recv_sem.at[k - 1],
            device_id={axis: peer},
            device_id_type=MESH,
        ).wait()
        return carry

    lax.fori_loop(1, n, finish, 0)


def exchange(x, axis, n, gather, cid):
    out_shape = ((n,) + x.shape) if gather else x.shape
    return pl.pallas_call(
        functools.partial(_exchange_kernel, axis, n, gather),
        out_shape=jax.ShapeDtypeStruct(out_shape, x.dtype),
        in_specs=[pl.BlockSpec(memory_space=pltpu.VMEM)],
        out_specs=pl.BlockSpec(memory_space=pltpu.VMEM),
        scratch_shapes=[
            pltpu.SemaphoreType.DMA((n - 1,)),
            pltpu.SemaphoreType.DMA((n - 1,)),
            pltpu.SemaphoreType.DMA,
        ],
        compiler_params=pltpu.CompilerParams(collective_id=cid, has_side_effects=True),
    )(x)


def _chip_facts(group):
    rep = lax.axis_index("rep")
    grp = lax.axis_index("grp")
    core = lax.rem(rep, 2)
    chip = lax.div(rep, 2) * group + grp
    partner = {"rep": rep + 1 - 2 * core}

    def device(c):
        return {"rep": lax.div(c, group) * 2 + core, "grp": lax.rem(c, group)}

    def block(c, k):
        return (lax.div(c, group) * 2 + k) * group + lax.rem(c, group)

    return core, chip, partner, device, block


def _greet_chips(chips, chip, partner, device):
    barrier = pltpu.get_barrier_semaphore()
    pl.semaphore_signal(barrier, inc=1, device_id=partner, device_id_type=MESH)

    def greet(k, carry):
        pl.semaphore_signal(
            barrier, inc=1, device_id=device(lax.rem(chip + k, chips)), device_id_type=MESH
        )
        return carry

    lax.fori_loop(1, chips, greet, 0)
    return barrier


def _gather_all_kernel(chips, group, x_ref, out_ref, send_sem, recv_sem, send2, recv2, own_sem):
    core, chip, partner, device, block = _chip_facts(group)
    barrier = _greet_chips(chips, chip, partner, device)
    mine = block(chip, core)
    own = pltpu.make_async_copy(x_ref, out_ref.at[mine], own_sem)
    own.start()
    pl.semaphore_wait(barrier, chips)

    def across(k, slot):
        return pltpu.make_async_remote_copy(
            src_ref=x_ref,
            dst_ref=out_ref.at[slot],
            send_sem=send_sem.at[k],
            recv_sem=recv_sem.at[k],
            device_id=device(lax.rem(chip + k, chips)),
            device_id_type=MESH,
        )

    def relay(k, slot):
        return pltpu.make_async_remote_copy(
            src_ref=out_ref.at[slot],
            dst_ref=out_ref.at[slot],
            send_sem=send2.at[k],
            recv_sem=recv2.at[k],
            device_id=partner,
            device_id_type=MESH,
        )

    def send(k, carry):
        across(k, mine).start()
        return carry

    lax.fori_loop(1, chips, send, 0)
    own.wait()
    relay(0, mine).start()

    def forward(k, carry):
        slot = block(lax.rem(chip + chips - k, chips), core)
        across(k, slot).wait_recv()
        relay(k, slot).start()
        return carry

    lax.fori_loop(1, chips, forward, 0)

    def finish(k, carry):
        source = lax.rem(chip + chips - k, chips)
        relay(k, block(source, 1 - core)).wait_recv()
        relay(k, block(source, core)).wait_send()
        return carry

    lax.fori_loop(0, chips, finish, 0)

    def drain(k, carry):
        across(k, mine).wait_send()
        return carry

    lax.fori_loop(1, chips, drain, 0)


def gather_all(x, rep_count, group, cid):
    chips = rep_count // 2 * group
    return pl.pallas_call(
        functools.partial(_gather_all_kernel, chips, group),
        out_shape=jax.ShapeDtypeStruct((rep_count * group,) + x.shape, x.dtype),
        in_specs=[pl.BlockSpec(memory_space=pltpu.VMEM)],
        out_specs=pl.BlockSpec(memory_space=pltpu.VMEM),
        scratch_shapes=[pltpu.SemaphoreType.DMA((chips,))] * 4 + [pltpu.SemaphoreType.DMA],
        compiler_params=pltpu.CompilerParams(collective_id=cid, has_side_effects=True),
    )(x)


def _reduce_all_kernel(
    chips, group, x_ref, base_ref, out_ref, pair_buf, send_buf, land, send1, recv1, send2, recv2
):
    core, chip, partner, device, block = _chip_facts(group)
    barrier = _greet_chips(chips, chip, partner, device)
    pl.semaphore_wait(barrier, chips)

    def to_partner(k):
        target = lax.rem(chip + k, chips)
        return pltpu.make_async_remote_copy(
            src_ref=x_ref.at[block(target, 1 - core)],
            dst_ref=pair_buf.at[k],
            send_sem=send1.at[k],
            recv_sem=recv1.at[k],
            device_id=partner,
            device_id_type=MESH,
        )

    def across(k):
        return pltpu.make_async_remote_copy(
            src_ref=send_buf.at[k],
            dst_ref=land.at[k],
            send_sem=send2.at[k],
            recv_sem=recv2.at[k],
            device_id=device(lax.rem(chip + k, chips)),
            device_id_type=MESH,
        )

    def start_pair(i, carry):
        to_partner(lax.rem(i, chips)).start()
        return carry

    lax.fori_loop(1, chips + 1, start_pair, 0)

    def add_pair(k, carry):
        to_partner(k).wait_recv()
        target = lax.rem(chip + k, chips)
        total = x_ref[block(target, core)].astype(jnp.float32) + pair_buf[k].astype(jnp.float32)
        send_buf[k] = total.astype(send_buf.dtype)

        @pl.when(k > 1)
        def _():
            across(k - 1).start()

        return carry

    lax.fori_loop(1, chips, add_pair, 0)
    to_partner(0).wait_recv()
    across(chips - 1).start()
    out_ref[...] = (
        base_ref[...].astype(jnp.float32)
        + x_ref[block(chip, core)].astype(jnp.float32)
        + pair_buf[0].astype(jnp.float32)
    )

    def take(k, carry):
        across(k).wait_recv()
        out_ref[...] += land[k].astype(jnp.float32)
        return carry

    lax.fori_loop(1, chips, take, 0)

    def drain(k, carry):
        to_partner(k).wait_send()

        @pl.when(k > 0)
        def _():
            across(k).wait_send()

        return carry

    lax.fori_loop(0, chips, drain, 0)


def reduce_all(x, base, rep_count, group, cid):
    chips = rep_count // 2 * group
    piece = x.shape[1:]
    return pl.pallas_call(
        functools.partial(_reduce_all_kernel, chips, group),
        out_shape=jax.ShapeDtypeStruct(piece, jnp.float32),
        in_specs=[pl.BlockSpec(memory_space=pltpu.VMEM)] * 2,
        out_specs=pl.BlockSpec(memory_space=pltpu.VMEM),
        scratch_shapes=[
            pltpu.VMEM((chips,) + piece, x.dtype),
            pltpu.VMEM((chips,) + piece, x.dtype),
            pltpu.VMEM((chips,) + piece, x.dtype),
        ]
        + [pltpu.SemaphoreType.DMA((chips,))] * 4,
        compiler_params=pltpu.CompilerParams(collective_id=cid, has_side_effects=True),
    )(x, base)


def norm_rows(resid, norm_gain):
    resid_f32 = resid.astype(jnp.float32)
    mean_sq = jnp.mean(resid_f32 * resid_f32, axis=1, keepdims=True)
    return (resid_f32 * lax.rsqrt(mean_sq + epsilon) * norm_gain.astype(jnp.float32)).astype(
        jnp.bfloat16
    )


def gated_rows(rows_in, gate_cols, up_cols):
    gate_val = jnp.dot(rows_in, gate_cols, preferred_element_type=jnp.float32)
    up_val = jnp.dot(rows_in, up_cols, preferred_element_type=jnp.float32)
    return (jax.nn.silu(gate_val) * up_val).astype(jnp.bfloat16)


def on_device(
    rep_count,
    group,
    hidden_in,
    q_nope,
    q_rope,
    new_kv,
    cache_kv,
    lengths,
    w_uk,
    w_uv,
    w_out,
    norm_gain,
    w_gate,
    w_up,
    w_down,
):
    seq_count = hidden_in.shape[0]
    heads_here = H // group
    slice_width = w_uk.shape[0]
    grp = lax.axis_index("grp")
    rep = lax.axis_index("rep")

    uv_own = lax.dynamic_slice_in_dim(w_uv, grp * heads_here * VH, heads_here * VH, 1)
    uv_parts = jnp.zeros((rep_count,) + uv_own.shape, uv_own.dtype)
    uv_parts = lax.dynamic_update_slice_in_dim(uv_parts, uv_own[None], rep, 0)
    for step in range(1, rep_count):
        moved = lax.ppermute(
            uv_own, "rep", [(i, (i + step) % rep_count) for i in range(rep_count)]
        )
        source = lax.rem(rep + rep_count - step, rep_count)
        uv_parts = lax.dynamic_update_slice_in_dim(uv_parts, moved[None], source, 0)
    value_up = uv_parts.reshape(KV_RANK, heads_here, VH)

    q_rows = exchange(q_nope.reshape(seq_count * H, NOPE), "rep", rep_count, True, 1)
    q_part = jnp.einsum(
        "bhd,chd->bhc",
        q_rows.reshape(rep_count * seq_count, H, NOPE),
        w_uk.reshape(slice_width, H, NOPE),
        preferred_element_type=jnp.float32,
    ).astype(jnp.bfloat16)
    q_back = exchange(
        q_part.reshape(rep_count, seq_count * H, slice_width), "rep", rep_count, False, 2
    )
    q_lat = q_back.reshape(rep_count, seq_count, H, slice_width)
    queries = jnp.concatenate(
        [q_lat[i] for i in range(rep_count)] + [q_rope.reshape(seq_count, H, ROPE)], axis=2
    )
    score_scale = float(NOPE + ROPE) ** (-0.5)
    scores = (
        jnp.einsum("bhc,blc->bhl", queries, cache_kv, preferred_element_type=jnp.float32)
        * score_scale
    )
    positions = lax.broadcasted_iota(jnp.int32, (1, 1, CACHE), 2)
    scores = jnp.where(positions < lengths[:, None, None], scores, -jnp.inf)
    own_score = (
        jnp.einsum("bhc,bc->bh", queries, new_kv, preferred_element_type=jnp.float32) * score_scale
    )
    row_top = jnp.maximum(jnp.max(scores, axis=2), own_score)
    weights = jnp.exp(scores - row_top[:, :, None])
    own_weight = jnp.exp(own_score - row_top)
    denom_sum = jnp.sum(weights, axis=2) + own_weight
    softmax_w = (weights / denom_sum[:, :, None]).astype(jnp.bfloat16)
    own_prob = (own_weight / denom_sum).astype(jnp.bfloat16)
    mixture = jnp.einsum("bhl,blc->bhc", softmax_w, cache_kv, preferred_element_type=jnp.float32)
    mixture = (
        mixture + own_prob.astype(jnp.float32)[:, :, None] * new_kv.astype(jnp.float32)[:, None, :]
    )
    latent = mixture[:, :, :KV_RANK].astype(jnp.bfloat16)

    by_heads = latent.reshape(seq_count, group, heads_here, KV_RANK).transpose(1, 0, 2, 3)
    latent_here = exchange(
        by_heads.reshape(group, seq_count * heads_here, KV_RANK), "grp", group, False, 3
    ).reshape(group * seq_count, heads_here, KV_RANK)
    head_out = jnp.einsum(
        "bhc,che->bhe", latent_here, value_up, preferred_element_type=jnp.float32
    ).astype(jnp.bfloat16)
    partial_value = jnp.dot(
        head_out.reshape(group * seq_count, heads_here * VH),
        w_out,
        preferred_element_type=jnp.float32,
    ).astype(jnp.bfloat16)
    pieces = exchange(
        partial_value.reshape(group, seq_count, partial_value.shape[1]), "grp", group, False, 4
    )
    resid_own = (
        hidden_in.astype(jnp.float32) + jnp.sum(pieces.astype(jnp.float32), axis=0)
    ).astype(jnp.bfloat16)
    normed = norm_rows(resid_own, norm_gain)
    every_row = gather_all(normed, rep_count, group, 5)
    every_row = every_row.reshape(rep_count * group * seq_count, -1)
    activated = gated_rows(every_row, w_gate, w_up)
    mlp_part = jnp.dot(activated, w_down, preferred_element_type=jnp.float32).astype(jnp.bfloat16)
    total = reduce_all(
        mlp_part.reshape(rep_count * group, seq_count, -1), resid_own, rep_count, group, 6
    )
    return total.astype(jnp.bfloat16)


def solution(mesh):
    return jax.shard_map(
        functools.partial(on_device, mesh.shape["rep"], mesh.shape["grp"]),
        mesh=mesh,
        in_specs=(
            P(("rep", "grp"), None),
            P(("rep", "grp"), None),
            P(("rep", "grp"), None),
            P(("rep", "grp"), None),
            P(("rep", "grp"), None, None),
            P(("rep", "grp")),
            P("rep", None),
            P("rep", None),
            P("grp", None),
            P(),
            P(None, ("rep", "grp")),
            P(None, ("rep", "grp")),
            P(("rep", "grp"), None),
        ),
        out_specs=P(("rep", "grp"), None),
        check_vma=False,
    )
```

time: 424 us -> 182 us (0.43)
  waiting for transfers between devices: 331 us -> 0.01 us
  Pallas kernels: 0 us -> 103 us
  between operations: 13.3 us -> 0.34 us
  matrix products: 59.6 us -> 49.3 us
  local copies, waits for them, and re-layouts: 6.89 us -> 17.1 us
    unnamed x6 -> x0, waiting for transfers between devices: 140 us -> none
    all_gather x3 -> x0, waiting for transfers between devices: 115 us -> none  [the longest x1 59.4 us: on_device(): lax.all_gather(w_uk, 'rep', axis=0, tiled=True)]
    pallas_call x0 -> x6, Pallas kernels: none -> 103 us  [the longest x4 46 us: exchange(): pl.pallas_call(functools.partial(_exchange_kernel, axis, n, gather), out_...]
    psum x1 -> x0, waiting for transfers between devices: 69 us -> none  [on_device(): summed = lax.psum(partial_value.astype(jnp.bfloat16), 'grp')]
    reshape x0 -> x4, local copies, waits for them, and re-layouts: none -> 9.7 us  [the longest x1 4.08 us: on_device(): mlp_part.reshape(rep_count * group, seq_count, -1)]
    dot_general x3, matrix products: 18.7 us -> 11.3 us  [the longest x1 7.86 us: on_device(): jnp.dot(head_out.reshape(group * seq_count, heads_here * VH), w_out, pref...]
    all_to_all x1 -> x0, waiting for transfers between devices: 6.86 us -> none  [on_device(): lax.all_to_all(head_out, 'grp', split_axis=1, concat_axis=0, tiled=True)]
    all_to_all x1 -> x0, starting transfers between devices: 5.51 us -> none  [on_device(): lax.all_to_all(head_out, 'grp', split_axis=1, concat_axis=0, tiled=True)]
  transfers between devices with their start and end apart: 6 -> 3, of which waited for: 6 -> 0; matrix products, arithmetic and copies ran while one was open for 7% -> 15% of each run, Pallas kernels for 0% -> 17%
where the time goes in v1:
time: 182 us; the launch traced here: 180 us
  Pallas kernels  103 us (57%)
  matrix products  49.3 us (27%)
  local copies, waits for them, and re-layouts  17.1 us (9%)
  other arithmetic  5.32 us (3%)
  starting transfers between devices  4.47 us (2%)
    pallas_call x4, Pallas kernels, exchange(): pl.pallas_call(functools.partial(_exchange_kernel, axis, n, gather), out_...  46 us
    pallas_call x1, Pallas kernels, reduce_all(): pl.pallas_call(functools.partial(_reduce_all_kernel, chips, group), out_s...  28.9 us
    pallas_call x1, Pallas kernels, gather_all(): pl.pallas_call(functools.partial(_gather_all_kernel, chips, group), out_s...  28.4 us
    dot_general x1, matrix products, on_device(): jnp.dot(activated, w_down, preferred_element_type=jnp.float32)  14.2 us
    dot_general x1, matrix products, on_device(): jnp.einsum('bhl,blc->bhc', softmax_w, cache_kv, preferred_element_type=jn...  9.59 us
    dot_general x1, matrix products, on_device(): jnp.einsum('bhc,blc->bhl', queries, cache_kv, preferred_element_type=jnp....  8.33 us
    dot_general x1, matrix products, on_device(): jnp.dot(head_out.reshape(group * seq_count, heads_here * VH), w_out, pref...  7.86 us
    dot_general x1, matrix products, gated_rows(): gate_val = jnp.dot(rows_in, gate_cols, preferred_element_type=jnp.float32)  5.63 us
  transfers between devices with their start and end apart: 3, of which 0 were waited for; matrix products, arithmetic and copies ran while one was open for 15% of the time, Pallas kernels for 17%

profile of v1, /device:TPU:0, one launch (start us, length us, event | category | flops | bytes accessed | tf_op | source)
XLA Modules:
  0.0 179.8 jit_solution(8486538681626386564)
XLA Ops:
  0.0 0.0 copy-start
  0.0 0.0 copy-start.5
  0.0 0.0 copy-start.8
  0.0 0.0 copy-start.7
  0.0 0.1 broadcast_in_dim.34
  0.1 1.8 %bitcast_dynamic-update-slice_fusion.3 = (bf16[4,128,1024]{2,1,0:T(8,128)(2,1)S(1)}, bf16[128,1024]{1,0:T(8,128)(2,1)}) fusion(bf16[4,128,1024]{2,1,0:T(8,128)(2,1)S(1)} %broadcast_in_dim.34, s32[]{:T(128)S(6)} %select_n.20, bf16[128,8192]{1,0:T(8,128)(2,1)} %param.20, s32[]{:T(128)S(6)} %select_n.19), kind=kLoop, calls=%fused_computation.32 | loop fusion | bytes 786440 | tf_op jit(solution)/shard_map/dynamic_update_slice | solution.py:314
  2.0 0.5 collective-permute-start
  2.5 2.5 %collective-permute-start.1 = (bf16[128,1024]{1,0:T(8,128)(2,1)}, bf16[128,1024]{1,0:T(8,128)(2,1)}, u32[]{:S(2)}, u32[]{:S(2)}) collective-permute-start(bf16[128,1024]{1,0:T(8,128)(2,1)} %get-tuple-element.8), channel_id=1, source_target_pairs={{0,16},{8,24},{16,0},{24,8},{1,17},{9,25},{17,1},{25,9},{2,18},{10... | collective-permute-start | bytes 786440 | tf_op jit(solution)/shard_map/ppermute | solution.py:316
  5.0 1.5 collective-permute-start.2
  6.5 1.6 reshape.84.x_ref
  8.0 12.5 %shard_map.127 = bf16[4,256,128]{2,1,0:T(8,128)(2,1)} custom-call(bf16[256,128]{1,0:T(8,128)(2,1)} %reshape.84.x_ref), custom_call_target="tpu_custom_call" | custom-call | tf_op jit(solution)/shard_map/pallas_call | solution.py:68
  20.5 0.0 copy-done
  20.5 2.1 %fusion.11 = bf16[16,64,128]{2,0,1:T(8,128)(2,1)S(1)} fusion(bf16[16,64,128]{2,1,0:T(8,128)(2,1)} %bitcast.60, bf16[128,8192]{1,0:T(8,128)(2,1)S(1)} %copy-done), kind=kOutput, calls=%fused_computation.15 | convolution fusion | flops 33685504 | bytes 2621440 | tf_op jit(solution)/shard_map/bhd,chd->bhc/dot_general | solution.py:324
  22.7 0.8 copy.21
  23.5 6.9 %shard_map.128 = bf16[4,256,128]{2,1,0:T(8,128)(2,1)} custom-call(bf16[4,256,128]{2,1,0:T(8,128)(2,1)} %bitcast.59), custom_call_target="tpu_custom_call" | custom-call | tf_op jit(solution)/shard_map/pallas_call | solution.py:68
  30.4 1.0 fusion.37
  31.4 0.0 copy-done.5
  31.4 0.1 reshape.87
  31.5 0.0 copy-done.8
  31.5 0.1 iota_compare_fusion
  31.7 0.0 copy-done.7
  31.7 0.2 fusion.32
  31.9 8.3 %fusion.38 = (f32[4,64]{1,0:T(4,128)S(1)}, f32[4,64,4096]{2,1,0:T(8,128)S(1)}) fusion(bf16[4,64,576]{2,1,0:T(8,128)(2,1)S(1)} %constant_dynamic-update-slice_fusion, bf16[4,4096,576]{1,2,0:T(8,128)(2,1)} %param.17, pred[4,4096]{1,0:T(4,128)(4,1)S(1)} %iota_compare_fusion), kind=kOutput, calls=%fused_computation.62 | convolution fusion | flops 1211105024 | bytes 23380992 | tf_op jit(solution)/shard_map/bhc,blc->bhl/dot_general | solution.py:339
  40.3 0.7 fusion.1
  41.0 0.0 copy-start.6
  41.0 9.6 %fusion.2 = f32[4,64,576]{2,1,0:T(8,128)S(1)} fusion(bf16[4,4096,576]{1,2,0:T(8,128)(2,1)} %param.17, f32[4,64,4096]{2,1,0:T(8,128)S(1)} %get-tuple-element.16, f32[4,64]{1,0:T(4,128)S(1)} %get-tuple-element.14, f32[4,64]{1,0:T(4,128)S(1)} %multiply_maximum_fusion), kind=kOutput, calls=%fused_computation.7 | convolution fusion | flops 1211105280 | bytes 23660544 | tf_op jit(solution)/shard_map/bhl,blc->bhc/dot_general | solution.py:353
  50.6 0.8 copy_bitcast_fusion.x_ref
  51.5 11.8 %shard_map.129 = bf16[8,32,512]{2,1,0:T(8,128)(2,1)} custom-call(bf16[8,32,512]{2,1,0:T(8,128)(2,1)} %copy_bitcast_fusion.x_ref), custom_call_target="tpu_custom_call" | custom-call | tf_op jit(solution)/shard_map/pallas_call | solution.py:68
  63.2 0.0 copy-done.6
  63.3 0.0 collective-permute-done
  63.3 1.0 bitcast_dynamic-update-slice_fusion.2
  64.2 0.0 collective-permute-done.1
  64.3 1.0 bitcast_dynamic-update-slice_fusion.1
  65.2 0.0 collective-permute-done.2
  65.3 0.3 copy.30
  65.5 1.3 fusion.15
  66.9 0.0 copy-start.4
  66.9 7.9 %convolution_convert_fusion.1 = bf16[32,7168]{1,0:T(8,128)(2,1)S(1)} fusion(bf16[1024,7168]{1,0:T(8,128)(2,1)} %param.21, bf16[8,4,8,128]{3,2,1,0:T(8,128)(2,1)S(1)} %fusion.15), kind=kOutput, calls=%fused_computation.1 | convolution fusion | flops 469991424 | bytes 15204352 | tf_op jit(solution)/shard_map/dot_general | solution.py:366
  74.7 0.9 reshape.92.x_ref
  75.7 14.8 %shard_map.130 = bf16[8,4,7168]{2,1,0:T(4,128)(2,1)} custom-call(bf16[8,4,7168]{2,1,0:T(4,128)(2,1)} %reshape.92.x_ref), custom_call_target="tpu_custom_call" | custom-call | tf_op jit(solution)/shard_map/pallas_call | solution.py:68
  90.4 1.2 convert_reduce_fusion
  91.7 0.0 copy-done.4
  91.7 0.2 fusion.27
  91.9 0.0 copy-start.3
  91.9 0.7 fusion.29.x_ref
  92.6 28.4 %shard_map.131 = bf16[32,4,7168]{2,1,0:T(4,128)(2,1)} custom-call(bf16[4,7168]{1,0:T(4,128)(2,1)} %fusion.29.x_ref), custom_call_target="tpu_custom_call" | custom-call | tf_op jit(solution)/shard_map/pallas_call | solution.py:173
  121.0 3.1 %reshape.93 = bf16[128,7168]{1,0:T(8,128)(2,1)S(1)} reshape(bf16[32,4,7168]{2,1,0:T(4,128)(2,1)} %shard_map.131) | data formatting | bytes 3670016 | tf_op jit(solution)/shard_map/reshape | solution.py:379
  124.1 0.0 copy-start.2
  124.1 1.2 copy-done.2
  125.4 5.6 %fusion.39 = f32[128,576]{0,1:T(8,128)S(1)} fusion(bf16[128,7168]{1,0:T(8,128)(2,1)S(1)} %reshape.93, bf16[7168,576]{0,1:T(8,128)(2,1)} %param.23), kind=kOutput, calls=%fused_computation.63 | convolution fusion | flops 1056964608 | bytes 10387456 | tf_op jit(solution)/shard_map/dot_general | solution.py:284
  131.0 0.0 copy-done.3
  131.0 0.0 copy-start.1
  131.0 14.2 %convolution_convert_fusion = bf16[128,7168]{1,0:T(8,128)(2,1)} fusion(bf16[576,7168]{1,0:T(8,128)(2,1)} %param.25, bf16[128,7168]{1,0:T(8,128)(2,1)} %copy-done.2, bf16[7168,576]{0,1:T(8,128)(2,1)} %param.24, f32[128,576]{0,1:T(8,128)S(1)} %fusion.39), kind=kOutput, calls=%fused_computation | convolution fusion | flops 2115289088 | bytes 20480000 | tf_op jit(solution)/shard_map/dot_general | solution.py:381
  145.2 4.1 %reshape.94.x_ref = bf16[32,4,7168]{2,1,0:T(4,128)(2,1)} reshape(bf16[128,7168]{1,0:T(8,128)(2,1)} %convolution_convert_fusion) | data formatting | bytes 3670016 | tf_op jit(solution)/shard_map/reshape | solution.py:383
  149.3 28.9 %shard_map.132 = f32[4,7168]{1,0:T(4,128)} custom-call(bf16[32,4,7168]{2,1,0:T(4,128)(2,1)} %reshape.94.x_ref, bf16[4,7168]{1,0:T(4,128)(2,1)} %copy-done.3), custom_call_target="tpu_custom_call" | custom-call | tf_op jit(solution)/shard_map/pallas_call | solution.py:260
  178.3 1.5 convert_element_type.72
  179.8 0.0 copy-done.1
  (11 shorter events, 0.1 us)
Async XLA Ops:
  0.0 20.5 %copy-start = (bf16[128,8192]{1,0:T(8,128)(2,1)S(1)}, bf16[128,8192]{1,0:T(8,128)(2,1)}, u32[]{:S(2)}) copy-start(bf16[128,8192]{1,0:T(8,128)(2,1)} %param.19) | copy-start | bytes 6291460
  0.0 31.4 %copy-start.5 = (bf16[4,4096]{1,0:T(4,128)(2,1)S(1)}, bf16[4,4096]{1,0:T(4,128)(2,1)}, u32[]{:S(2)}) copy-start(bf16[4,4096]{1,0:T(4,128)(2,1)} %param.15) | copy-start | bytes 98308
  0.0 31.5 %copy-start.8 = (s32[4]{0:T(128)S(1)}, s32[4]{0:T(128)}, u32[]{:S(2)}) copy-start(s32[4]{0:T(128)} %param.18) | copy-start | bytes 52
  0.0 31.7 %copy-start.7 = (bf16[4,576]{1,0:T(4,128)(2,1)S(1)}, bf16[4,576]{1,0:T(4,128)(2,1)}, u32[]{:S(2)}) copy-start(bf16[4,576]{1,0:T(4,128)(2,1)} %param.16) | copy-start | bytes 13828
  2.0 61.3 %collective-permute-start = (bf16[128,1024]{1,0:T(8,128)(2,1)}, bf16[128,1024]{1,0:T(8,128)(2,1)}, u32[]{:S(2)}, u32[]{:S(2)}) collective-permute-start(bf16[128,1024]{1,0:T(8,128)(2,1)} %get-tuple-element.8), channel_id=1, source_target_pairs={{0,8},{8,16},{16,24},{24,0},{1,9},{9,17},{17,25},{25,1},{2,10},{10... | collective-permute-start | bytes 786440 | tf_op jit(solution)/shard_map/ppermute | solution.py:316
  2.5 61.8 %collective-permute-start.1 = (bf16[128,1024]{1,0:T(8,128)(2,1)}, bf16[128,1024]{1,0:T(8,128)(2,1)}, u32[]{:S(2)}, u32[]{:S(2)}) collective-permute-start(bf16[128,1024]{1,0:T(8,128)(2,1)} %get-tuple-element.8), channel_id=1, source_target_pairs={{0,16},{8,24},{16,0},{24,8},{1,17},{9,25},{17,1},{25,9},{2,18},{10... | collective-permute-start | bytes 786440 | tf_op jit(solution)/shard_map/ppermute | solution.py:316
  5.0 60.2 %collective-permute-start.2 = (bf16[128,1024]{1,0:T(8,128)(2,1)}, bf16[128,1024]{1,0:T(8,128)(2,1)S(1)}, u32[]{:S(2)}, u32[]{:S(2)}) collective-permute-start(bf16[128,1024]{1,0:T(8,128)(2,1)} %get-tuple-element.8), channel_id=1, source_target_pairs={{0,24},{8,0},{16,8},{24,16},{1,25},{9,1},{17,9},{25,17},{2,26},{10... | collective-permute-start | bytes 786440 | tf_op jit(solution)/shard_map/ppermute | solution.py:316
  41.0 22.2 %copy-start.6 = (bf16[7168]{0:T(1024)(128)(2,1)S(1)}, bf16[7168]{0:T(1024)(128)(2,1)}, u32[]{:S(2)}) copy-start(bf16[7168]{0:T(1024)(128)(2,1)} %param.22) | copy-start | bytes 43012
  66.9 24.8 %copy-start.4 = (bf16[4,7168]{1,0:T(4,128)(2,1)S(1)}, bf16[4,7168]{1,0:T(4,128)(2,1)}, u32[]{:S(2)}) copy-start(bf16[4,7168]{1,0:T(4,128)(2,1)} %param.13) | copy-start | bytes 172036
  91.9 39.1 %copy-start.3 = (bf16[4,7168]{1,0:T(4,128)(2,1)}, bf16[4,7168]{1,0:T(4,128)(2,1)S(1)}, u32[]{:S(2)}) copy-start(bf16[4,7168]{1,0:T(4,128)(2,1)S(1)} %get-tuple-element.6.base_ref) | copy-start | bytes 172036
  124.1 1.2 copy-start.2
  131.0 48.8 %copy-start.1 = (bf16[128,8192]{1,0:T(8,128)(2,1)S(1)}, bf16[128,8192]{1,0:T(8,128)(2,1)}, u32[]{:S(2)}) copy-start(bf16[128,8192]{1,0:T(8,128)(2,1)} %param.19) | copy-start | bytes 6291460

commit v2 on v0

v2 whole, which is shorter than its diff:
```python
import functools

import jax
import jax.numpy as jnp
from jax import lax
from jax.experimental import pallas as pl
from jax.experimental.pallas import tpu as pltpu
from jax.sharding import PartitionSpec as P

H = 64
NOPE = 128
ROPE = 64
VH = 128
KV_RANK = 512
CACHE = 4096
MESH = pl.DeviceIdType.MESH

epsilon = 1e-06


def _exchange_kernel(axis, n, gather, x_ref, out_ref, send_sem, recv_sem, own_sem):
    me = lax.axis_index(axis)
    barrier = pltpu.get_barrier_semaphore()

    def greet(k, carry):
        peer = lax.rem(me + k, n)
        pl.semaphore_signal(barrier, inc=1, device_id={axis: peer}, device_id_type=MESH)
        return carry

    lax.fori_loop(1, n, greet, 0)
    own = pltpu.make_async_copy(x_ref if gather else x_ref.at[me], out_ref.at[me], own_sem)
    own.start()
    pl.semaphore_wait(barrier, n - 1)

    def send(k, carry):
        peer = lax.rem(me + k, n)
        pltpu.make_async_remote_copy(
            src_ref=x_ref if gather else x_ref.at[peer],
            dst_ref=out_ref.at[me],
            send_sem=send_sem.at[k - 1],
            recv_sem=recv_sem.at[k - 1],
            device_id={axis: peer},
            device_id_type=MESH,
        ).start()
        return carry

    lax.fori_loop(1, n, send, 0)
    own.wait()

    def finish(k, carry):
        source = lax.rem(me + n - k, n)
        peer = lax.rem(me + k, n)
        pltpu.make_async_remote_copy(
            src_ref=x_ref if gather else x_ref.at[peer],
            dst_ref=out_ref.at[source],
            send_sem=send_sem.at[k - 1],
            recv_sem=recv_sem.at[k - 1],
            device_id={axis: peer},
            device_id_type=MESH,
        ).wait()
        return carry

    lax.fori_loop(1, n, finish, 0)


def exchange(x, axis, n, gather, cid):
    out_shape = ((n,) + x.shape) if gather else x.shape
    return pl.pallas_call(
        functools.partial(_exchange_kernel, axis, n, gather),
        out_shape=jax.ShapeDtypeStruct(out_shape, x.dtype),
        in_specs=[pl.BlockSpec(memory_space=pltpu.VMEM)],
        out_specs=pl.BlockSpec(memory_space=pltpu.VMEM),
        scratch_shapes=[
            pltpu.SemaphoreType.DMA((n - 1,)),
            pltpu.SemaphoreType.DMA((n - 1,)),
            pltpu.SemaphoreType.DMA,
        ],
        compiler_params=pltpu.CompilerParams(collective_id=cid, has_side_effects=True),
    )(x)


def _pair_kernel(h_ref, r_ref, h_out, r_out, send_sem, recv_sem, own_sem):
    rep = lax.axis_index("rep")
    core = lax.rem(rep, 2)
    partner = {"rep": rep + 1 - 2 * core}
    barrier = pltpu.get_barrier_semaphore()
    pl.semaphore_signal(barrier, inc=1, device_id=partner, device_id_type=MESH)
    own = [
        pltpu.make_async_copy(src, dst.at[core], own_sem.at[i])
        for i, (src, dst) in enumerate(((h_ref, h_out), (r_ref, r_out)))
    ]
    for copy in own:
        copy.start()
    pl.semaphore_wait(barrier, 1)

    def remote(i, src, dst, slot):
        return pltpu.make_async_remote_copy(
            src_ref=src,
            dst_ref=dst.at[slot],
            send_sem=send_sem.at[i],
            recv_sem=recv_sem.at[i],
            device_id=partner,
            device_id_type=MESH,
        )

    remote(0, h_ref, h_out, core).start()
    remote(1, r_ref, r_out, core).start()
    for copy in own:
        copy.wait()
    remote(0, h_ref, h_out, 1 - core).wait()
    remote(1, r_ref, r_out, 1 - core).wait()


def pair_gather(heads, resid, cid):
    vmem = pl.BlockSpec(memory_space=pltpu.VMEM)
    return pl.pallas_call(
        _pair_kernel,
        out_shape=[jax.ShapeDtypeStruct((2,) + v.shape, v.dtype) for v in (heads, resid)],
        in_specs=[vmem] * 2,
        out_specs=[vmem] * 2,
        scratch_shapes=[pltpu.SemaphoreType.DMA((2,))] * 3,
        compiler_params=pltpu.CompilerParams(collective_id=cid, has_side_effects=True),
    )(heads, resid)


def _half_product_kernel(core_ref, x_ref, w_ref, out_ref):
    out_ref[...] = jnp.dot(x_ref[...], w_ref[...], preferred_element_type=jnp.float32).astype(
        out_ref.dtype
    )


def half_product(core, x, w):
    rows, depth = x.shape
    half = w.shape[1] // 2
    tile = half // 7
    return pl.pallas_call(
        _half_product_kernel,
        out_shape=jax.ShapeDtypeStruct((rows, half), x.dtype),
        grid_spec=pltpu.PrefetchScalarGridSpec(
            num_scalar_prefetch=1,
            grid=(7,),
            in_specs=[
                pl.BlockSpec((rows, depth), lambda i, core: (0, 0)),
                pl.BlockSpec((depth, tile), lambda i, core: (0, core[0] * 7 + i)),
            ],
            out_specs=pl.BlockSpec((rows, tile), lambda i, core: (0, i)),
        ),
    )(core, x, w)


def _mlp_kernel(
    zs,
    part,
    hid,
    gain,
    wg_hbm,
    wu_hbm,
    wd_hbm,
    out,
    wg,
    wu,
    wd,
    ra,
    sz,
    rz,
    ssq_out,
    ssq_in,
    rows,
    acc_g,
    acc_u,
    act,
    pout,
    pin,
    own,
    sb,
    rb,
    sa2,
    ra2,
    sz2,
    rz2,
    resid,
    w_sem,
    a_s,
    a_r,
    z_s,
    z_r,
    q_s,
    q_r,
    gz_s,
    gz_r,
    ga_s,
    ga_r,
    gb_s,
    gb_r,
    gp_s,
    gp_r,
    t_s,
    t_r,
    b2_s,
    b2_r,
    a2_s,
    a2_r,
    z2_s,
    z2_r,
    f_s,
    f_r,
):
    rep = lax.axis_index("rep")
    grp = lax.axis_index("grp")
    core = lax.rem(rep, 2)
    y = lax.div(rep, 2)
    z = lax.div(grp, 2)
    x = lax.rem(grp, 2)
    half = part.shape[2]
    tile = half // 7
    own_cols = pl.ds(pl.multiple_of(core * half, 128), half)
    far_cols = pl.ds(pl.multiple_of((1 - core) * half, 128), half)
    f32 = jnp.float32

    weights = [
        pltpu.make_async_copy(src, dst, w_sem.at[i])
        for i, (src, dst) in enumerate(((wg_hbm, wg), (wu_hbm, wu), (wd_hbm, wd)))
    ]
    for copy in weights:
        copy.start()

    def at(k):
        return lax.rem(z + k, zs)

    def device(k, dx, dy):
        return {
            "rep": (y + dy * (1 - 2 * y)) * 2 + core,
            "grp": at(k) * 2 + x + dx * (1 - 2 * x),
        }

    def block(k, da, db):
        dx = da * (1 - core) + db * core
        dy = db * (1 - core) + da * core
        return ((y + dy * (1 - 2 * y)) * zs + at(k)) * 2 + x + dx * (1 - 2 * x)

    a_dev = device(0, 1 - core, core)
    b_dev = device(0, core, 1 - core)
    x_dev = device(0, 1, 0)
    partner = {"rep": rep + 1 - 2 * core, "grp": grp}

    def copy_to(src, dst, s, r, dev):
        return pltpu.make_async_remote_copy(
            src_ref=src, dst_ref=dst, send_sem=s, recv_sem=r, device_id=dev, device_id_type=MESH
        )

    barrier = pltpu.get_barrier_semaphore()
    for dev in (partner, a_dev, b_dev):
        pl.semaphore_signal(barrier, inc=1, device_id=dev, device_id_type=MESH)

    def loop(low, high, body):
        def step(i, carry):
            body(i)
            return carry

        lax.fori_loop(low, high, step, 0)

    loop(
        1,
        zs,
        lambda k: pl.semaphore_signal(
            barrier, inc=1, device_id=device(k, 0, 0), device_id_type=MESH
        ),
    )
    pl.semaphore_wait(barrier, zs + 2)

    def to_x(k):
        return copy_to(
            part.at[at(k) * 2 + 1 - x], ra.at[at(k)], a_s.at[at(k)], a_r.at[at(k)], x_dev
        )

    loop(1, zs + 1, lambda k: to_x(k).start())

    def to_z(k):
        return copy_to(sz.at[k], rz.at[k], z_s.at[k], z_r.at[k], device(k, 0, 0))

    def sum_x(k):
        to_x(k).wait_recv()
        sz[k] = (part[at(k) * 2 + x].astype(f32) + ra[at(k)].astype(f32)).astype(sz.dtype)

        @pl.when(k > 1)
        def _():
            to_z(k - 1).start()

    loop(1, zs, sum_x)
    to_x(0).wait_recv()
    resid[...] = hid[...].astype(f32) + part[z * 2 + x].astype(f32) + ra[z].astype(f32)
    to_z(zs - 1).start()

    def sum_z(k):
        to_z(k).wait_recv()
        resid[...] += rz[k].astype(f32)

    loop(1, zs, sum_z)
    rounded = resid[...].astype(hid.dtype).astype(f32)
    resid[...] = rounded
    ssq = jnp.sum(rounded * rounded, axis=1, keepdims=True)
    ssq_out[...] = jnp.broadcast_to(ssq, ssq_out.shape)
    to_q = copy_to(ssq_out, ssq_in, q_s, q_r, partner)
    to_q.start()
    to_q.wait()
    mean_sq = (ssq + ssq_in[:, 0:1]) / (2 * half)
    mine = block(0, 0, 0)
    rows[mine, :, own_cols] = (
        resid[...] * lax.rsqrt(mean_sq + epsilon) * gain[...].astype(f32)
    ).astype(rows.dtype)

    def piece(k, da, db):
        return rows.at[block(zs - k, da, db), :, own_cols]

    def gather_z(k, source):
        return copy_to(
            piece(source, 0, 0), piece(source, 0, 0), gz_s.at[k], gz_r.at[k], device(k, 0, 0)
        )

    def gather_a(k, da):
        return copy_to(piece(k, da, 0), piece(k, da, 0), ga_s.at[k], ga_r.at[k], a_dev)

    def gather_b(k, da, db):
        j = da * zs + k
        return copy_to(piece(k, da, db), piece(k, da, db), gb_s.at[j], gb_r.at[j], b_dev)

    def relay(k, da, db, cols):
        j = k * 4 + da * (2 - core) + db * (1 + core)
        ref = rows.at[block(zs - k, da, db), :, cols]
        return copy_to(ref, ref, gp_s.at[j], gp_r.at[j], partner)

    loop(1, zs, lambda k: gather_z(k, 0).start())
    gather_b(0, 0, 0).start()
    gather_a(0, 0).start()
    relay(0, 0, 0, own_cols).start()

    def from_z(k):
        gather_z(k, k).wait_recv()
        gather_b(k, 0, 0).start()
        gather_a(k, 0).start()
        relay(k, 0, 0, own_cols).start()

    loop(1, zs, from_z)

    def from_a(k):
        gather_a(k, 1).wait_recv()
        gather_b(k, 1, 0).start()
        relay(k, 1, 0, own_cols).start()

    loop(0, zs, from_a)

    def from_b(j):
        da = lax.div(j, zs)
        k = lax.rem(j, zs)
        gather_b(k, da, 1).wait_recv()
        relay(k, da, 1, own_cols).start()

    loop(0, 2 * zs, from_b)

    def from_partner(j):
        da = lax.rem(lax.div(j, 2), 2)
        db = lax.rem(j, 2)
        relay(lax.div(j, 4), da, db, far_cols).wait_recv()

    loop(0, 4 * zs, from_partner)

    count = rows.shape[0] * rows.shape[1]
    depth = rows.shape[2] // 7
    weights[0].wait()
    weights[1].wait()
    acc_g[...] = jnp.zeros_like(acc_g)
    acc_u[...] = jnp.zeros_like(acc_u)

    def project(i):
        cols = pl.ds(pl.multiple_of(i * depth, 128), depth)
        lhs = rows[:, :, cols].reshape(count, depth)
        acc_g[...] += jnp.dot(lhs, wg[cols, :], preferred_element_type=f32)
        acc_u[...] += jnp.dot(lhs, wu[cols, :], preferred_element_type=f32)

    loop(0, 7, project)
    act[...] = (jax.nn.silu(acc_g[...]) * acc_u[...]).astype(act.dtype)
    weights[2].wait()

    def to_partner(i):
        return copy_to(pout.at[i], pin.at[i], t_s.at[i], t_r.at[i], partner)

    def down(first, i):
        cols = pl.ds(pl.multiple_of(first * half + i * tile, 128), tile)
        return jnp.dot(act[...], wd[:, cols], preferred_element_type=f32)

    def down_far(i):
        pout[i] = down(1 - core, i).astype(pout.dtype).reshape(pout.shape[1:])

        @pl.when(i > 0)
        def _():
            to_partner(i - 1).start()

    loop(0, 7, down_far)
    own[0] = down(core, 0).reshape(own.shape[1:])
    to_partner(6).start()

    def down_own(i):
        own[i] = down(core, i).reshape(own.shape[1:])
        to_partner(i - 1).wait_recv()
        own[i - 1] += pin[i - 1].astype(f32)

    loop(1, 7, down_own)
    to_partner(6).wait_recv()
    own[6] += pin[6].astype(f32)

    def value(k, da, db):
        target = block(k, da, db)
        return jnp.concatenate([own[i, target] for i in range(7)], axis=1)

    def to_b(j):
        return copy_to(sb.at[j], rb.at[j], b2_s.at[j], b2_r.at[j], b_dev)

    def slot(i):
        return (1 - lax.div(i, zs)) * zs + lax.rem(lax.rem(i, zs) + 1, zs)

    def sum_b(i):
        j = slot(i)
        sb[j] = value(lax.rem(j, zs), lax.div(j, zs), 1).astype(sb.dtype)

        @pl.when(i > 0)
        def _():
            to_b(slot(i - 1)).start()

    loop(0, 2 * zs, sum_b)
    to_b(0).start()

    def to_a(k):
        return copy_to(sa2.at[k], ra2.at[k], a2_s.at[k], a2_r.at[k], a_dev)

    def sum_a(i):
        k = lax.rem(i + 1, zs)
        to_b(zs + k).wait_recv()
        sa2[k] = (value(k, 1, 0) + rb[zs + k].astype(f32)).astype(sa2.dtype)

        @pl.when(i > 0)
        def _():
            to_a(i).start()

    loop(0, zs, sum_a)
    to_a(0).start()

    def to_z2(k):
        return copy_to(sz2.at[k], rz2.at[k], z2_s.at[k], z2_r.at[k], device(k, 0, 0))

    def so_far(k):
        to_b(k).wait_recv()
        to_a(k).wait_recv()
        return value(k, 0, 0) + rb[k].astype(f32) + ra2[k].astype(f32)

    def sum_z2(k):
        sz2[k] = so_far(k).astype(sz2.dtype)

        @pl.when(k > 1)
        def _():
            to_z2(k - 1).start()

    loop(1, zs, sum_z2)
    resid[...] += so_far(0)
    to_z2(zs - 1).start()

    def take_z2(k):
        to_z2(k).wait_recv()
        resid[...] += rz2[k].astype(f32)

    loop(1, zs, take_z2)
    out[:, own_cols] = resid[...].astype(out.dtype)

    def final(cols):
        return copy_to(out.at[:, cols], out.at[:, cols], f_s, f_r, partner)

    final(own_cols).start()

    loop(1, zs + 1, lambda k: to_x(k).wait_send())
    loop(0, 7, lambda i: to_partner(i).wait_send())

    def drain_z(k):
        to_z(k).wait_send()
        gather_z(k, 0).wait_send()
        to_z2(k).wait_send()

    loop(1, zs, drain_z)

    def drain_a(k):
        gather_a(k, 0).wait_send()
        to_a(k).wait_send()

    loop(0, zs, drain_a)

    def drain_b(j):
        gather_b(lax.rem(j, zs), lax.div(j, zs), 0).wait_send()
        to_b(j).wait_send()

    loop(0, 2 * zs, drain_b)

    def drain_relay(j):
        da = lax.rem(lax.div(j, 2), 2)
        relay(lax.div(j, 4), da, lax.rem(j, 2), own_cols).wait_send()

    loop(0, 4 * zs, drain_relay)
    final(far_cols).wait_recv()
    final(own_cols).wait_send()


def mlp_all(part, hid, gain, w_gate, w_up, w_down, group, cid):
    zs = group // 2
    eight, half = part.shape[1:]
    width = 2 * half
    hidden = w_gate.shape[1]
    count = 4 * zs * eight
    bf16, f32 = jnp.bfloat16, jnp.float32
    vmem = pl.BlockSpec(memory_space=pltpu.VMEM)
    hbm = pl.BlockSpec(memory_space=pltpu.HBM)

    def blocks(n):
        return pltpu.VMEM((n, eight, half), bf16)

    def sems(*counts):
        return [pltpu.SemaphoreType.DMA((n,)) for n in counts for _ in range(2)]

    one = [pltpu.SemaphoreType.DMA, pltpu.SemaphoreType.DMA]
    return pl.pallas_call(
        functools.partial(_mlp_kernel, zs),
        out_shape=jax.ShapeDtypeStruct((eight, width), bf16),
        in_specs=[vmem] * 3 + [hbm] * 3,
        out_specs=vmem,
        scratch_shapes=[
            pltpu.VMEM((width, hidden), bf16),
            pltpu.VMEM((width, hidden), bf16),
            pltpu.VMEM((hidden, width), bf16),
            blocks(zs),
            blocks(zs),
            blocks(zs),
            pltpu.VMEM((eight, 128), f32),
            pltpu.VMEM((eight, 128), f32),
            pltpu.VMEM((4 * zs, eight, width), bf16),
            pltpu.VMEM((count, hidden), f32),
            pltpu.VMEM((count, hidden), f32),
            pltpu.VMEM((count, hidden), bf16),
            pltpu.VMEM((7, 4 * zs, eight, half // 7), bf16),
            pltpu.VMEM((7, 4 * zs, eight, half // 7), bf16),
            pltpu.VMEM((7, 4 * zs, eight, half // 7), f32),
            blocks(2 * zs),
            blocks(2 * zs),
            blocks(zs),
            blocks(zs),
            blocks(zs),
            blocks(zs),
            pltpu.VMEM((eight, half), f32),
            pltpu.SemaphoreType.DMA((3,)),
        ]
        + sems(zs, zs)
        + one
        + sems(zs, zs, 2 * zs, 4 * zs, 7, 2 * zs, zs, zs)
        + one,
        compiler_params=pltpu.CompilerParams(
            collective_id=cid, has_side_effects=True, vmem_limit_bytes=60 * 1024 * 1024
        ),
    )(part, hid, gain, w_gate, w_up, w_down)


def on_device(
    rep_count,
    group,
    hidden_in,
    q_nope,
    q_rope,
    new_kv,
    cache_kv,
    lengths,
    w_uk,
    w_uv,
    w_out,
    norm_gain,
    w_gate,
    w_up,
    w_down,
):
    seq_count = hidden_in.shape[0]
    heads_here = H // group
    slice_width = w_uk.shape[0]
    grp = lax.axis_index("grp")
    rep = lax.axis_index("rep")

    q_rows = exchange(q_nope.reshape(seq_count * H, NOPE), "rep", rep_count, True, 1)
    q_part = jnp.einsum(
        "bhd,chd->bhc",
        q_rows.reshape(rep_count * seq_count, H, NOPE),
        w_uk.reshape(slice_width, H, NOPE),
        preferred_element_type=jnp.float32,
    ).astype(jnp.bfloat16)
    q_back = exchange(
        q_part.reshape(rep_count, seq_count * H, slice_width), "rep", rep_count, False, 2
    )
    uv_own = lax.dynamic_slice_in_dim(w_uv, grp * heads_here * VH, heads_here * VH, 1)
    uv_own, q_back = lax.optimization_barrier((uv_own, q_back))
    uv_parts = jnp.zeros((rep_count,) + uv_own.shape, uv_own.dtype)
    uv_parts = lax.dynamic_update_slice_in_dim(uv_parts, uv_own[None], rep, 0)
    for step in range(1, rep_count):
        moved = lax.ppermute(
            uv_own, "rep", [(i, (i + step) % rep_count) for i in range(rep_count)]
        )
        source = lax.rem(rep + rep_count - step, rep_count)
        uv_parts = lax.dynamic_update_slice_in_dim(uv_parts, moved[None], source, 0)
    value_up = uv_parts.reshape(KV_RANK, heads_here, VH)

    q_lat = q_back.reshape(rep_count, seq_count, H, slice_width)
    queries = jnp.concatenate(
        [q_lat[i] for i in range(rep_count)] + [q_rope.reshape(seq_count, H, ROPE)], axis=2
    )
    score_scale = float(NOPE + ROPE) ** (-0.5)
    scores = (
        jnp.einsum("bhc,blc->bhl", queries, cache_kv, preferred_element_type=jnp.float32)
        * score_scale
    )
    positions = lax.broadcasted_iota(jnp.int32, (1, 1, CACHE), 2)
    scores = jnp.where(positions < lengths[:, None, None], scores, -jnp.inf)
    own_score = (
        jnp.einsum("bhc,bc->bh", queries, new_kv, preferred_element_type=jnp.float32) * score_scale
    )
    row_top = jnp.maximum(jnp.max(scores, axis=2), own_score)
    weights = jnp.exp(scores - row_top[:, :, None])
    own_weight = jnp.exp(own_score - row_top)
    denom_sum = jnp.sum(weights, axis=2) + own_weight
    softmax_w = (weights / denom_sum[:, :, None]).astype(jnp.bfloat16)
    own_prob = (own_weight / denom_sum).astype(jnp.bfloat16)
    mixture = jnp.einsum("bhl,blc->bhc", softmax_w, cache_kv, preferred_element_type=jnp.float32)
    mixture = (
        mixture + own_prob.astype(jnp.float32)[:, :, None] * new_kv.astype(jnp.float32)[:, None, :]
    )
    latent = mixture[:, :, :KV_RANK].astype(jnp.bfloat16)

    by_heads = latent.reshape(seq_count, group, heads_here, KV_RANK).transpose(1, 0, 2, 3)
    latent_here = exchange(
        by_heads.reshape(group, seq_count * heads_here, KV_RANK), "grp", group, False, 3
    ).reshape(group * seq_count, heads_here, KV_RANK)
    head_out = jnp.einsum(
        "bhc,che->bhe", latent_here, value_up, preferred_element_type=jnp.float32
    ).astype(jnp.bfloat16)
    core = lax.rem(rep, 2)
    half = w_out.shape[1] // 2
    head_pair, hidden_pair = pair_gather(
        head_out.reshape(group * seq_count, heads_here * VH), hidden_in, 4
    )
    chip_rows = (
        head_pair.reshape(2, group, seq_count, -1)
        .transpose(1, 0, 2, 3)
        .reshape(group * 2 * seq_count, -1)
    )
    part = half_product(jnp.full((1,), core, jnp.int32), chip_rows, w_out)
    hid = lax.dynamic_slice_in_dim(hidden_pair.reshape(2 * seq_count, -1), core * half, half, 1)
    gain = lax.dynamic_slice_in_dim(norm_gain[None], core * half, half, 1)
    total = mlp_all(
        part.reshape(group, 2 * seq_count, half), hid, gain, w_gate, w_up, w_down, group, 5
    )
    return lax.dynamic_slice_in_dim(total, core * seq_count, seq_count, 0)


def solution(mesh):
    return jax.shard_map(
        functools.partial(on_device, mesh.shape["rep"], mesh.shape["grp"]),
        mesh=mesh,
        in_specs=(
            P(("rep", "grp"), None),
            P(("rep", "grp"), None),
            P(("rep", "grp"), None),
            P(("rep", "grp"), None),
            P(("rep", "grp"), None, None),
            P(("rep", "grp")),
            P("rep", None),
            P("rep", None),
            P("grp", None),
            P(),
            P(None, ("rep", "grp")),
            P(None, ("rep", "grp")),
            P(("rep", "grp"), None),
        ),
        out_specs=P(("rep", "grp"), None),
        check_vma=False,
    )
```

time: 424 us -> 157 us (0.37)
  waiting for transfers between devices: 331 us -> 0.01 us
  Pallas kernels: 0 us -> 95.1 us
  matrix products: 59.6 us -> 20.6 us
  local copies, waits for them, and re-layouts: 6.89 us -> 36.1 us
  between operations: 13.3 us -> 0.29 us
  other arithmetic: 6.88 us -> 1.63 us
    unnamed x6 -> x0, waiting for transfers between devices: 140 us -> none
    all_gather x3 -> x0, waiting for transfers between devices: 115 us -> none  [the longest x1 59.4 us: on_device(): lax.all_gather(w_uk, 'rep', axis=0, tiled=True)]
    pallas_call x0 -> x6, Pallas kernels: none -> 95.1 us  [the longest x1 58.3 us: mlp_all(): pl.pallas_call(functools.partial(_mlp_kernel, zs), out_shape=jax.ShapeDty...]
    psum x1 -> x0, waiting for transfers between devices: 69 us -> none  [on_device(): summed = lax.psum(partial_value.astype(jnp.bfloat16), 'grp')]
    dot_general x5 -> x2, matrix products: 39.2 us -> 2.49 us  [the longest x1 2.13 us: on_device(): jnp.einsum('bhd,chd->bhc', q_rows.reshape(rep_count * seq_count, H, NOPE)...]
    unnamed x20 -> x21, local copies, waits for them, and re-layouts: 6.7 us -> 25.2 us
    all_to_all x1 -> x0, waiting for transfers between devices: 6.86 us -> none  [on_device(): lax.all_to_all(head_out, 'grp', split_axis=1, concat_axis=0, tiled=True)]
    all_to_all x1 -> x0, starting transfers between devices: 5.51 us -> none  [on_device(): lax.all_to_all(head_out, 'grp', split_axis=1, concat_axis=0, tiled=True)]
  transfers between devices with their start and end apart: 6 -> 3, of which waited for: 6 -> 0; matrix products, arithmetic and copies ran while one was open for 7% -> 30% of each run, Pallas kernels for 0% -> 8%
where the time goes in v2:
time: 157 us; the launch traced here: 156 us
  Pallas kernels  95.1 us (61%)
  local copies, waits for them, and re-layouts  36.1 us (23%)
  matrix products  20.6 us (13%)
  starting transfers between devices  2.33 us (1%)
  other arithmetic  1.63 us (1%)
    pallas_call x1, Pallas kernels, mlp_all(): pl.pallas_call(functools.partial(_mlp_kernel, zs), out_shape=jax.ShapeDty...  58.3 us
    pallas_call x3, Pallas kernels, exchange(): pl.pallas_call(functools.partial(_exchange_kernel, axis, n, gather), out_...  26.8 us
    unnamed x21, local copies, waits for them, and re-layouts  25.2 us
    dot_general x1, matrix products, on_device(): jnp.einsum('bhl,blc->bhc', softmax_w, cache_kv, preferred_element_type=jn...  9.59 us
    dot_general x1, matrix products, on_device(): jnp.einsum('bhc,blc->bhl', queries, cache_kv, preferred_element_type=jnp....  8.34 us
    pallas_call x1, Pallas kernels, half_product(): pl.pallas_call(_half_product_kernel, out_shape=jax.ShapeDtypeStruct((rows...  7.01 us
  transfers between devices with their start and end apart: 3, of which 0 were waited for; matrix products, arithmetic and copies ran while one was open for 30% of the time, Pallas kernels for 8%

profile of v2, /device:TPU:0, one launch (start us, length us, event | category | flops | bytes accessed | tf_op | source)
XLA Modules:
  0.0 156.1 jit_solution(11120818580095636243)
XLA Ops:
  0.0 0.0 copy-start
  0.0 0.0 copy-start.4
  0.0 0.0 copy-start.6
  0.0 0.0 copy-start.3
  0.0 1.7 %reshape.78.x_ref = bf16[256,128]{1,0:T(8,128)(2,1)} reshape(bf16[4,8192]{1,0:T(4,128)(2,1)} %param.14) | data formatting | bytes 131072 | tf_op jit(solution)/shard_map/reshape | solution.py:589
  1.7 7.9 %shard_map.127 = bf16[4,256,128]{2,1,0:T(8,128)(2,1)} custom-call(bf16[256,128]{1,0:T(8,128)(2,1)} %reshape.78.x_ref), custom_call_target="tpu_custom_call" | custom-call | tf_op jit(solution)/shard_map/pallas_call | solution.py:68
  9.6 0.0 copy-done
  9.6 2.1 %fusion.11 = bf16[16,64,128]{2,0,1:T(8,128)(2,1)S(1)} fusion(bf16[16,64,128]{2,1,0:T(8,128)(2,1)} %bitcast.61, bf16[128,8192]{1,0:T(8,128)(2,1)S(1)} %copy-done), kind=kOutput, calls=%fused_computation.12 | convolution fusion | flops 33685504 | bytes 2621440 | tf_op jit(solution)/shard_map/bhd,chd->bhc/dot_general | solution.py:590
  11.8 0.8 copy.25
  12.6 7.0 %shard_map.128 = bf16[4,256,128]{2,1,0:T(8,128)(2,1)} custom-call(bf16[4,256,128]{2,1,0:T(8,128)(2,1)} %bitcast.59), custom_call_target="tpu_custom_call" | custom-call | tf_op jit(solution)/shard_map/pallas_call | solution.py:68
  19.5 1.0 constant_dynamic-slice_fusion.2
  20.5 1.9 %collective-permute-start.2 = (bf16[128,1024]{1,0:T(8,128)(2,1)S(1)}, bf16[128,1024]{1,0:T(8,128)(2,1)S(1)}, u32[]{:S(2)}, u32[]{:S(2)}) collective-permute-start(bf16[128,1024]{1,0:T(8,128)(2,1)S(1)} %constant_dynamic-slice_fusion.2), channel_id=1, source_target_pairs={{0,24},{8,0},{16,8},{24,16},{1,25},{9,1},{17,9},{25,17},{2,26},{10... | collective-permute-start | bytes 786440 | tf_op jit(solution)/shard_map/ppermute | solution.py:604
  22.5 0.4 collective-permute-start.1
  22.9 0.0 collective-permute-start
  22.9 0.0 copy-done.4
  22.9 0.0 copy-done.6
  22.9 0.1 iota_compare_fusion
  23.0 0.0 copy-done.3
  23.0 0.1 reshape.82
  23.1 1.0 fusion.24
  24.2 0.2 fusion.20
  24.4 8.3 %fusion.25 = (f32[4,64]{1,0:T(4,128)S(1)}, f32[4,64,4096]{2,1,0:T(8,128)S(1)}) fusion(bf16[4,64,576]{2,1,0:T(8,128)(2,1)S(1)} %constant_dynamic-update-slice_fusion, bf16[4,4096,576]{1,2,0:T(8,128)(2,1)} %param.17, pred[4,4096]{1,0:T(4,128)(4,1)S(1)} %iota_compare_fusion), kind=kOutput, calls=%fused_computation.45 | convolution fusion | flops 1211105024 | bytes 23380992 | tf_op jit(solution)/shard_map/bhc,blc->bhl/dot_general | solution.py:617
  32.7 0.7 fusion.1
  33.5 0.0 copy-start.5
  33.5 9.6 %fusion.2 = f32[4,64,576]{2,1,0:T(8,128)S(1)} fusion(bf16[4,4096,576]{1,2,0:T(8,128)(2,1)} %param.17, f32[4,64,4096]{2,1,0:T(8,128)S(1)} %get-tuple-element.20, f32[4,64]{1,0:T(4,128)S(1)} %get-tuple-element.18, f32[4,64]{1,0:T(4,128)S(1)} %multiply_maximum_fusion), kind=kOutput, calls=%fused_computation.5 | convolution fusion | flops 1211105280 | bytes 23660544 | tf_op jit(solution)/shard_map/bhl,blc->bhc/dot_general | solution.py:631
  43.1 0.8 copy_bitcast_fusion.x_ref
  43.9 0.1 broadcast_in_dim.37
  44.1 0.0 copy-done.5
  44.1 0.1 dynamic-slice.3
  44.2 0.6 dynamic_slice.14.gain
  44.8 12.0 %shard_map.129 = bf16[8,32,512]{2,1,0:T(8,128)(2,1)} custom-call(bf16[8,32,512]{2,1,0:T(8,128)(2,1)} %copy_bitcast_fusion.x_ref), custom_call_target="tpu_custom_call" | custom-call | tf_op jit(solution)/shard_map/pallas_call | solution.py:68
  56.7 12.4 %copy.31.wg_hbm = bf16[7168,576]{1,0:T(8,128)(2,1)} copy(bf16[7168,576]{0,1:T(8,128)(2,1)} %param.23) | data formatting | bytes 16515072 | tf_op args[10]
  69.2 0.0 copy-start.2
  69.2 12.4 %copy.32.wu_hbm = bf16[7168,576]{1,0:T(8,128)(2,1)} copy(bf16[7168,576]{0,1:T(8,128)(2,1)} %param.24) | data formatting | bytes 16515072 | tf_op args[11]
  81.5 0.0 collective-permute-done
  81.6 0.0 collective-permute-done.1
  81.6 0.0 collective-permute-done.2
  81.7 0.3 copy.37
  81.9 0.0 copy-done.2
  81.9 0.4 fusion.14
  82.3 0.6 copy.58
  82.9 2.9 %shard_map.130 = (bf16[2,32,1024]{2,1,0:T(8,128)(2,1)}, bf16[2,4,7168]{2,1,0:T(4,128)(2,1)}) custom-call(bf16[32,1024]{1,0:T(8,128)(2,1)} %bitcast.63, bf16[4,7168]{1,0:T(4,128)(2,1)} %r_ref.1), custom_call_target="tpu_custom_call" | custom-call | tf_op jit(solution)/shard_map/pallas_call | solution.py:116
  85.9 1.0 reshape.87
  86.9 0.7 reshape.88.x_ref
  87.6 0.9 reshape.90
  88.5 0.6 constant_dynamic-slice_fusion.1.hid
  89.1 7.0 %shard_map.131 = bf16[64,3584]{1,0:T(8,128)(2,1)} custom-call(s32[1]{0:T(128)} %bitcast.core_ref, bf16[64,1024]{1,0:T(8,128)(2,1)} %reshape.88.x_ref, bf16[1024,7168]{1,0:T(8,128)(2,1)} %w_ref.1), custom_call_target="tpu_custom_call" | custom-call | tf_op jit(solution)/shard_map/pallas_call | solution.py:136
  96.2 0.0 copy-start.1
  96.2 58.3 %shard_map.132 = bf16[8,7168]{1,0:T(8,128)(2,1)} custom-call(bf16[8,8,3584]{2,1,0:T(8,128)(2,1)} %bitcast.57, bf16[8,3584]{1,0:T(8,128)(2,1)} %constant_dynamic-slice_fusion.1.hid, bf16[1,3584]{1,0:T(2,128)(2,1)} %dynamic_slice.14.gain, bf16[7168,576]{1,0:T(8,128)(2,1)} %copy.31.wg_hbm, bf16[7168,576]{1,0:T(8,128)(2,1)} %copy.32.wu_hbm, bf16[576,7168]{1,0:T(8,128)(2,1)} %wd_hbm.1), custom_call_target="tpu_custom_call" | custom-call | tf_op jit(solution)/shard_map/pallas_call | solution.py:526
  154.5 1.6 constant_dynamic-slice_fusion
  156.1 0.0 copy-done.1
  (13 shorter events, 0.3 us)
Async XLA Ops:
  0.0 9.6 %copy-start = (bf16[128,8192]{1,0:T(8,128)(2,1)S(1)}, bf16[128,8192]{1,0:T(8,128)(2,1)}, u32[]{:S(2)}) copy-start(bf16[128,8192]{1,0:T(8,128)(2,1)} %param.19) | copy-start | bytes 6291460
  0.0 22.9 %copy-start.4 = (bf16[4,576]{1,0:T(4,128)(2,1)S(1)}, bf16[4,576]{1,0:T(4,128)(2,1)}, u32[]{:S(2)}) copy-start(bf16[4,576]{1,0:T(4,128)(2,1)} %param.16) | copy-start | bytes 13828
  0.0 22.9 %copy-start.6 = (s32[4]{0:T(128)S(1)}, s32[4]{0:T(128)}, u32[]{:S(2)}) copy-start(s32[4]{0:T(128)} %param.18) | copy-start | bytes 52
  0.0 23.0 %copy-start.3 = (bf16[4,4096]{1,0:T(4,128)(2,1)S(1)}, bf16[4,4096]{1,0:T(4,128)(2,1)}, u32[]{:S(2)}) copy-start(bf16[4,4096]{1,0:T(4,128)(2,1)} %param.15) | copy-start | bytes 98308
  20.5 61.1 %collective-permute-start.2 = (bf16[128,1024]{1,0:T(8,128)(2,1)S(1)}, bf16[128,1024]{1,0:T(8,128)(2,1)S(1)}, u32[]{:S(2)}, u32[]{:S(2)}) collective-permute-start(bf16[128,1024]{1,0:T(8,128)(2,1)S(1)} %constant_dynamic-slice_fusion.2), channel_id=1, source_target_pairs={{0,24},{8,0},{16,8},{24,16},{1,25},{9,1},{17,9},{25,17},{2,26},{10... | collective-permute-start | bytes 786440 | tf_op jit(solution)/shard_map/ppermute | solution.py:604
  22.5 59.1 %collective-permute-start.1 = (bf16[128,1024]{1,0:T(8,128)(2,1)S(1)}, bf16[128,1024]{1,0:T(8,128)(2,1)S(1)}, u32[]{:S(2)}, u32[]{:S(2)}) collective-permute-start(bf16[128,1024]{1,0:T(8,128)(2,1)S(1)} %constant_dynamic-slice_fusion.2), channel_id=1, source_target_pairs={{0,16},{8,24},{16,0},{24,8},{1,17},{9,25},{17,1},{25,9},{2,18},{10... | collective-permute-start | bytes 786440 | tf_op jit(solution)/shard_map/ppermute | solution.py:604
  22.9 58.7 %collective-permute-start = (bf16[128,1024]{1,0:T(8,128)(2,1)S(1)}, bf16[128,1024]{1,0:T(8,128)(2,1)S(1)}, u32[]{:S(2)}, u32[]{:S(2)}) collective-permute-start(bf16[128,1024]{1,0:T(8,128)(2,1)S(1)} %constant_dynamic-slice_fusion.2), channel_id=1, source_target_pairs={{0,8},{8,16},{16,24},{24,0},{1,9},{9,17},{17,25},{25,1},{2,10},{10... | collective-permute-start | bytes 786440 | tf_op jit(solution)/shard_map/ppermute | solution.py:604
  33.5 10.6 %copy-start.5 = (bf16[7168]{0:T(1024)(128)(2,1)S(1)}, bf16[7168]{0:T(1024)(128)(2,1)}, u32[]{:S(2)}) copy-start(bf16[7168]{0:T(1024)(128)(2,1)} %param.22) | copy-start | bytes 43012
  69.2 12.8 %copy-start.2 = (bf16[8,32,512]{2,1,0:T(8,128)(2,1)S(1)}, bf16[8,32,512]{2,1,0:T(8,128)(2,1)}, u32[]{:S(2)}) copy-start(bf16[8,32,512]{2,1,0:T(8,128)(2,1)} %shard_map.129) | copy-start | bytes 786436
  96.2 59.9 %copy-start.1 = (bf16[128,8192]{1,0:T(8,128)(2,1)S(1)}, bf16[128,8192]{1,0:T(8,128)(2,1)}, u32[]{:S(2)}) copy-start(bf16[128,8192]{1,0:T(8,128)(2,1)} %param.19) | copy-start | bytes 6291460

commit v3 on v2

--- a/solution.py
+++ b/solution.py
@@ -14,6 +14,7 @@
 KV_RANK = 512
 CACHE = 4096
 MESH = pl.DeviceIdType.MESH
+ROWS = (((1,), (1,)), ((), ()))
 
 epsilon = 1e-06
 
@@ -374,8 +375,8 @@
     def project(i):
         cols = pl.ds(pl.multiple_of(i * depth, 128), depth)
         lhs = rows[:, :, cols].reshape(count, depth)
-        acc_g[...] += jnp.dot(lhs, wg[cols, :], preferred_element_type=f32)
-        acc_u[...] += jnp.dot(lhs, wu[cols, :], preferred_element_type=f32)
+        acc_g[...] += lax.dot_general(lhs, wg[:, cols], ROWS, preferred_element_type=f32)
+        acc_u[...] += lax.dot_general(lhs, wu[:, cols], ROWS, preferred_element_type=f32)
 
     loop(0, 7, project)
     act[...] = (jax.nn.silu(acc_g[...]) * acc_u[...]).astype(act.dtype)
@@ -510,7 +511,7 @@
     zs = group // 2
     eight, half = part.shape[1:]
     width = 2 * half
-    hidden = w_gate.shape[1]
+    hidden = w_gate.shape[0]
     count = 4 * zs * eight
     bf16, f32 = jnp.bfloat16, jnp.float32
     vmem = pl.BlockSpec(memory_space=pltpu.VMEM)
@@ -529,8 +530,8 @@
         in_specs=[vmem] * 3 + [hbm] * 3,
         out_specs=vmem,
         scratch_shapes=[
-            pltpu.VMEM((width, hidden), bf16),
-            pltpu.VMEM((width, hidden), bf16),
+            pltpu.VMEM((hidden, width), bf16),
+            pltpu.VMEM((hidden, width), bf16),
             pltpu.VMEM((hidden, width), bf16),
             blocks(zs),
             blocks(zs),
@@ -563,6 +564,71 @@
     )(part, hid, gain, w_gate, w_up, w_down)
 
 
+def _attend_kernel(tile, lengths, q_ref, new_ref, cache_ref, out_ref, top, denom, acc):
+    b = pl.program_id(0)
+    j = pl.program_id(1)
+    f32 = jnp.float32
+    scale = float(NOPE + ROPE) ** (-0.5)
+
+    @pl.when(j == 0)
+    def _():
+        own = q_ref[0].astype(f32) * new_ref[0].astype(f32)
+        top[...] = jnp.sum(own, axis=1, keepdims=True) * scale
+        denom[...] = jnp.ones_like(denom)
+        acc[...] = jnp.broadcast_to(new_ref[0][:, :KV_RANK].astype(f32), acc.shape)
+
+    @pl.when(j * tile < lengths[b])
+    def _():
+        cache = cache_ref[0]
+        scores = jnp.dot(q_ref[0], cache, preferred_element_type=f32) * scale
+        positions = j * tile + lax.broadcasted_iota(jnp.int32, (1, tile), 1)
+        scores = jnp.where(positions < lengths[b], scores, -jnp.inf)
+        new_top = jnp.maximum(top[...], jnp.max(scores, axis=1, keepdims=True))
+        weights = jnp.exp(scores - new_top)
+        shrink = jnp.exp(top[...] - new_top)
+        denom[...] = shrink * denom[...] + jnp.sum(weights, axis=1, keepdims=True)
+        acc[...] = shrink * acc[...] + lax.dot_general(
+            weights.astype(cache.dtype), cache[:KV_RANK], ROWS, preferred_element_type=f32
+        )
+        top[...] = new_top
+
+    @pl.when(j == pl.num_programs(1) - 1)
+    def _():
+        out_ref[0] = (acc[...] / denom[...]).astype(out_ref.dtype)
+
+
+def attend(lengths, queries, new_kv, cache_kv):
+    seq_count, length, width = cache_kv.shape
+    tile = length // 4
+    return pl.pallas_call(
+        functools.partial(_attend_kernel, tile),
+        out_shape=jax.ShapeDtypeStruct((seq_count, H, KV_RANK), queries.dtype),
+        grid_spec=pltpu.PrefetchScalarGridSpec(
+            num_scalar_prefetch=1,
+            grid=(seq_count, 4),
+            in_specs=[
+                pl.BlockSpec((1, H, width), lambda b, j, n: (b, 0, 0)),
+                pl.BlockSpec((1, 1, width), lambda b, j, n: (b, 0, 0)),
+                pl.BlockSpec(
+                    (1, width, tile),
+                    lambda b, j, n: (b, 0, jnp.minimum(j, lax.div(n[b] - 1, tile))),
+                ),
+            ],
+            out_specs=pl.BlockSpec((1, H, KV_RANK), lambda b, j, n: (b, 0, 0)),
+            scratch_shapes=[
+                pltpu.VMEM((H, 1), jnp.float32),
+                pltpu.VMEM((H, 1), jnp.float32),
+                pltpu.VMEM((H, KV_RANK), jnp.float32),
+            ],
+        ),
+        cost_estimate=pl.CostEstimate(
+            flops=4 * seq_count * H * length * width,
+            bytes_accessed=2 * cache_kv.size,
+            transcendentals=seq_count * H * length,
+        ),
+    )(lengths, queries, new_kv.reshape(seq_count, 1, width), jnp.swapaxes(cache_kv, 1, 2))
+
+
 def on_device(
     rep_count,
     group,
@@ -612,27 +678,7 @@
     queries = jnp.concatenate(
         [q_lat[i] for i in range(rep_count)] + [q_rope.reshape(seq_count, H, ROPE)], axis=2
     )
-    score_scale = float(NOPE + ROPE) ** (-0.5)
-    scores = (
-        jnp.einsum("bhc,blc->bhl", queries, cache_kv, preferred_element_type=jnp.float32)
-        * score_scale
-    )
-    positions = lax.broadcasted_iota(jnp.int32, (1, 1, CACHE), 2)
-    scores = jnp.where(positions < lengths[:, None, None], scores, -jnp.inf)
-    own_score = (
-        jnp.einsum("bhc,bc->bh", queries, new_kv, preferred_element_type=jnp.float32) * score_scale
-    )
-    row_top = jnp.maximum(jnp.max(scores, axis=2), own_score)
-    weights = jnp.exp(scores - row_top[:, :, None])
-    own_weight = jnp.exp(own_score - row_top)
-    denom_sum = jnp.sum(weights, axis=2) + own_weight
-    softmax_w = (weights / denom_sum[:, :, None]).astype(jnp.bfloat16)
-    own_prob = (own_weight / denom_sum).astype(jnp.bfloat16)
-    mixture = jnp.einsum("bhl,blc->bhc", softmax_w, cache_kv, preferred_element_type=jnp.float32)
-    mixture = (
-        mixture + own_prob.astype(jnp.float32)[:, :, None] * new_kv.astype(jnp.float32)[:, None, :]
-    )
-    latent = mixture[:, :, :KV_RANK].astype(jnp.bfloat16)
+    latent = attend(lengths, queries, new_kv, cache_kv)
 
     by_heads = latent.reshape(seq_count, group, heads_here, KV_RANK).transpose(1, 0, 2, 3)
     latent_here = exchange(
@@ -655,7 +701,7 @@
     hid = lax.dynamic_slice_in_dim(hidden_pair.reshape(2 * seq_count, -1), core * half, half, 1)
     gain = lax.dynamic_slice_in_dim(norm_gain[None], core * half, half, 1)
     total = mlp_all(
-        part.reshape(group, 2 * seq_count, half), hid, gain, w_gate, w_up, w_down, group, 5
+        part.reshape(group, 2 * seq_count, half), hid, gain, w_gate.T, w_up.T, w_down, group, 5
     )
     return lax.dynamic_slice_in_dim(total, core * seq_count, seq_count, 0)
 

time: 157 us -> 135 us (0.86)
  local copies, waits for them, and re-layouts: 36.1 us -> 14.3 us
  Pallas kernels: 95.1 us -> 114 us
  matrix products: 20.6 us -> 2.5 us
  other arithmetic: 1.63 us -> 0 us
    unnamed x21 -> x19, local copies, waits for them, and re-layouts: 25.2 us -> 1.08 us
    dot_general x3 -> x0, matrix products: 18.1 us -> none  [the longest x1 9.59 us: on_device(): jnp.einsum('bhl,blc->bhc', softmax_w, cache_kv, preferred_element_type=jn...]
    pallas_call x0 -> x1, Pallas kernels: none -> 17.6 us  [attend(): pl.pallas_call(functools.partial(_attend_kernel, tile), out_shape=jax.Sha...]
    reshape x0 -> x2, local copies, waits for them, and re-layouts: none -> 2.29 us  [the longest x1 1.68 us: on_device(): by_heads.reshape(group, seq_count * heads_here, KV_RANK)]
    pallas_call x3, Pallas kernels: 26.8 us -> 28.5 us  [exchange(): pl.pallas_call(functools.partial(_exchange_kernel, axis, n, gather), out_...]
  transfers between devices with their start and end apart: 3 -> 3, of which waited for: 0 -> 0; matrix products, arithmetic and copies ran while one was open for 30% -> 3% of each run, Pallas kernels for 8% -> 23%
where the time goes in v3:
time: 135 us
  Pallas kernels  114 us (84%)
  local copies, waits for them, and re-layouts  14.3 us (11%)
  starting transfers between devices  3.14 us (2%)
  matrix products  2.5 us (2%)
    pallas_call x1, Pallas kernels, mlp_all(): pl.pallas_call(functools.partial(_mlp_kernel, zs), out_shape=jax.ShapeDty...  58.4 us
    pallas_call x3, Pallas kernels, exchange(): pl.pallas_call(functools.partial(_exchange_kernel, axis, n, gather), out_...  28.5 us
    pallas_call x1, Pallas kernels, attend(): pl.pallas_call(functools.partial(_attend_kernel, tile), out_shape=jax.Sha...  17.6 us
    pallas_call x1, Pallas kernels, half_product(): pl.pallas_call(_half_product_kernel, out_shape=jax.ShapeDtypeStruct((rows...  7 us
    ppermute x3, starting transfers between devices, on_device(): lax.ppermute(uv_own, 'rep', [(i, (i + step) % rep_count) for i in range(r...  3.14 us
    pallas_call x1, Pallas kernels, pair_gather(): pl.pallas_call(_pair_kernel, out_shape=[jax.ShapeDtypeStruct((2,) + v.sha...  2.94 us
  transfers between devices with their start and end apart: 3, of which 0 were waited for; matrix products, arithmetic and copies ran while one was open for 3% of the time, Pallas kernels for 23%

profile of v3, /device:TPU:0, one launch (start us, length us, event | category | flops | bytes accessed | tf_op | source)
XLA Modules:
  0.0 134.6 jit_solution(17279297070855559394)
XLA Ops:
  0.0 0.0 copy-start
  0.0 1.7 %reshape.56.x_ref = bf16[256,128]{1,0:T(8,128)(2,1)} reshape(bf16[4,8192]{1,0:T(4,128)(2,1)} %param.14) | data formatting | bytes 131072 | tf_op jit(solution)/shard_map/reshape | solution.py:655
  1.7 7.9 %shard_map.127 = bf16[4,256,128]{2,1,0:T(8,128)(2,1)} custom-call(bf16[256,128]{1,0:T(8,128)(2,1)} %reshape.56.x_ref), custom_call_target="tpu_custom_call" | custom-call | tf_op jit(solution)/shard_map/pallas_call | solution.py:69
  9.6 0.0 copy-done
  9.6 0.0 copy-start.4
  9.6 0.0 copy-start.5
  9.7 2.1 %fusion.6 = bf16[16,64,128]{2,0,1:T(8,128)(2,1)S(1)} fusion(bf16[16,64,128]{2,1,0:T(8,128)(2,1)} %bitcast.61, bf16[128,8192]{1,0:T(8,128)(2,1)S(1)} %copy-done), kind=kOutput, calls=%fused_computation.4 | convolution fusion | flops 33685504 | bytes 2621440 | tf_op jit(solution)/shard_map/bhd,chd->bhc/dot_general | solution.py:656
  11.8 0.8 copy.23
  12.6 6.9 %shard_map.128 = bf16[4,256,128]{2,1,0:T(8,128)(2,1)} custom-call(bf16[4,256,128]{2,1,0:T(8,128)(2,1)} %bitcast.59), custom_call_target="tpu_custom_call" | custom-call | tf_op jit(solution)/shard_map/pallas_call | solution.py:69
  19.6 1.0 constant_dynamic-slice_fusion.2
  20.5 0.7 collective-permute-start
  21.2 1.6 %collective-permute-start.1 = (bf16[128,1024]{1,0:T(8,128)(2,1)S(1)}, bf16[128,1024]{1,0:T(8,128)(2,1)S(1)}, u32[]{:S(2)}, u32[]{:S(2)}) collective-permute-start(bf16[128,1024]{1,0:T(8,128)(2,1)S(1)} %constant_dynamic-slice_fusion.2), channel_id=1, source_target_pairs={{0,16},{8,24},{16,0},{24,8},{1,17},{9,25},{17,1},{25,9},{2,18},{10... | collective-permute-start | bytes 786440 | tf_op jit(solution)/shard_map/ppermute | solution.py:670
  22.9 0.8 collective-permute-start.2
  23.7 1.0 fusion.13
  24.7 0.0 copy-done.4
  24.7 0.1 reshape.60
  24.8 0.0 copy-done.5
  24.8 0.6 copy.24.new_ref
  25.5 0.0 copy-start.2
  25.5 0.7 copy-done.2
  26.2 17.6 %shard_map.129 = bf16[4,64,512]{2,1,0:T(8,128)(2,1)} custom-call(s32[4]{0:T(128)} %lengths.1, bf16[4,64,576]{2,1,0:T(8,128)(2,1)} %copy-done.2, bf16[4,1,576]{2,1,0:T(2,128)(2,1)} %copy.24.new_ref, bf16[4,576,4096]{2,1,0:T(8,128)(2,1)} %bitcast.53), custom_call_target="tpu_custom_call" | custom-call | flops 2415919104 | bytes 18874368 | tf_op jit(solution)/shard_map/pallas_call | solution.py:603
  43.8 0.0 copy-start.6
  43.8 1.7 %copy_bitcast_fusion.x_ref = bf16[8,32,512]{2,1,0:T(8,128)(2,1)} fusion(bf16[4,64,512]{2,1,0:T(8,128)(2,1)} %shard_map.129), kind=kLoop, calls=%fused_computation.13 | loop fusion | bytes 524288 | tf_op jit(solution)/shard_map/reshape | solution.py:685
  45.5 0.1 broadcast_in_dim.20
  45.7 13.6 %shard_map.130 = bf16[8,32,512]{2,1,0:T(8,128)(2,1)} custom-call(bf16[8,32,512]{2,1,0:T(8,128)(2,1)} %copy_bitcast_fusion.x_ref), custom_call_target="tpu_custom_call" | custom-call | tf_op jit(solution)/shard_map/pallas_call | solution.py:69
  59.3 0.0 copy-start.3
  59.3 0.0 copy-done.6
  59.3 0.1 dynamic-slice.3
  59.4 0.6 dynamic_slice.14.gain
  60.0 0.0 collective-permute-done
  60.0 0.0 collective-permute-done.1
  60.1 0.0 collective-permute-done.2
  60.1 0.3 copy.32
  60.4 0.0 copy-done.3
  60.4 0.4 fusion.9
  60.8 0.6 copy.51
  61.4 2.9 %shard_map.131 = (bf16[2,32,1024]{2,1,0:T(8,128)(2,1)}, bf16[2,4,7168]{2,1,0:T(4,128)(2,1)}) custom-call(bf16[32,1024]{1,0:T(8,128)(2,1)} %bitcast.63, bf16[4,7168]{1,0:T(4,128)(2,1)} %r_ref.1), custom_call_target="tpu_custom_call" | custom-call | tf_op jit(solution)/shard_map/pallas_call | solution.py:117
  64.3 1.0 reshape.66
  65.4 0.7 reshape.67.x_ref
  66.0 0.9 reshape.69
  67.0 0.6 constant_dynamic-slice_fusion.1.hid
  67.6 7.0 %shard_map.132 = bf16[64,3584]{1,0:T(8,128)(2,1)} custom-call(s32[1]{0:T(128)} %bitcast.core_ref, bf16[64,1024]{1,0:T(8,128)(2,1)} %reshape.67.x_ref, bf16[1024,7168]{1,0:T(8,128)(2,1)} %w_ref.1), custom_call_target="tpu_custom_call" | custom-call | tf_op jit(solution)/shard_map/pallas_call | solution.py:137
  74.6 0.0 copy-start.1
  74.6 58.4 %shard_map.133 = bf16[8,7168]{1,0:T(8,128)(2,1)} custom-call(bf16[8,8,3584]{2,1,0:T(8,128)(2,1)} %bitcast.57, bf16[8,3584]{1,0:T(8,128)(2,1)} %constant_dynamic-slice_fusion.1.hid, bf16[1,3584]{1,0:T(2,128)(2,1)} %dynamic_slice.14.gain, bf16[576,7168]{1,0:T(8,128)(2,1)} %bitcast.54, bf16[576,7168]{1,0:T(8,128)(2,1)} %bitcast.55, bf16[576,7168]{1,0:T(8,128)(2,1)} %wd_hbm.1), custom_call_target="tpu_custom_call" | custom-call | tf_op jit(solution)/shard_map/pallas_call | solution.py:527
  133.0 1.6 %constant_dynamic-slice_fusion = bf16[4,7168]{1,0:T(4,128)(2,1)} fusion(bf16[8,7168]{1,0:T(8,128)(2,1)} %shard_map.133, s32[]{:T(128)S(6)} %select_n.28), kind=kLoop, calls=%fused_computation.22 | loop fusion | bytes 114692 | tf_op jit(solution)/shard_map/dynamic_slice | solution.py:706
  134.5 0.0 copy-done.1
  (10 shorter events, 0.2 us)
Async XLA Ops:
  0.0 9.6 %copy-start = (bf16[128,8192]{1,0:T(8,128)(2,1)S(1)}, bf16[128,8192]{1,0:T(8,128)(2,1)}, u32[]{:S(2)}) copy-start(bf16[128,8192]{1,0:T(8,128)(2,1)} %param.19) | copy-start | bytes 6291460
  9.6 15.0 %copy-start.4 = (bf16[4,4096]{1,0:T(4,128)(2,1)S(1)}, bf16[4,4096]{1,0:T(4,128)(2,1)}, u32[]{:S(2)}) copy-start(bf16[4,4096]{1,0:T(4,128)(2,1)} %param.15) | copy-start | bytes 98308
  9.6 15.1 %copy-start.5 = (bf16[4,576]{1,0:T(4,128)(2,1)S(1)}, bf16[4,576]{1,0:T(4,128)(2,1)}, u32[]{:S(2)}) copy-start(bf16[4,576]{1,0:T(4,128)(2,1)} %param.16) | copy-start | bytes 13828
  20.5 39.4 %collective-permute-start = (bf16[128,1024]{1,0:T(8,128)(2,1)S(1)}, bf16[128,1024]{1,0:T(8,128)(2,1)S(1)}, u32[]{:S(2)}, u32[]{:S(2)}) collective-permute-start(bf16[128,1024]{1,0:T(8,128)(2,1)S(1)} %constant_dynamic-slice_fusion.2), channel_id=1, source_target_pairs={{0,8},{8,16},{16,24},{24,0},{1,9},{9,17},{17,25},{25,1},{2,10},{10... | collective-permute-start | bytes 786440 | tf_op jit(solution)/shard_map/ppermute | solution.py:670
  21.2 38.8 %collective-permute-start.1 = (bf16[128,1024]{1,0:T(8,128)(2,1)S(1)}, bf16[128,1024]{1,0:T(8,128)(2,1)S(1)}, u32[]{:S(2)}, u32[]{:S(2)}) collective-permute-start(bf16[128,1024]{1,0:T(8,128)(2,1)S(1)} %constant_dynamic-slice_fusion.2), channel_id=1, source_target_pairs={{0,16},{8,24},{16,0},{24,8},{1,17},{9,25},{17,1},{25,9},{2,18},{10... | collective-permute-start | bytes 786440 | tf_op jit(solution)/shard_map/ppermute | solution.py:670
  22.9 37.2 %collective-permute-start.2 = (bf16[128,1024]{1,0:T(8,128)(2,1)S(1)}, bf16[128,1024]{1,0:T(8,128)(2,1)S(1)}, u32[]{:S(2)}, u32[]{:S(2)}) collective-permute-start(bf16[128,1024]{1,0:T(8,128)(2,1)S(1)} %constant_dynamic-slice_fusion.2), channel_id=1, source_target_pairs={{0,24},{8,0},{16,8},{24,16},{1,25},{9,1},{17,9},{25,17},{2,26},{10... | collective-permute-start | bytes 786440 | tf_op jit(solution)/shard_map/ppermute | solution.py:670
  25.5 0.7 copy-start.2
  43.8 15.5 %copy-start.6 = (bf16[7168]{0:T(1024)(128)(2,1)S(1)}, bf16[7168]{0:T(1024)(128)(2,1)}, u32[]{:S(2)}) copy-start(bf16[7168]{0:T(1024)(128)(2,1)} %param.22) | copy-start | bytes 43012
  59.3 1.1 copy-start.3
  74.6 60.0 %copy-start.1 = (bf16[128,8192]{1,0:T(8,128)(2,1)S(1)}, bf16[128,8192]{1,0:T(8,128)(2,1)}, u32[]{:S(2)}) copy-start(bf16[128,8192]{1,0:T(8,128)(2,1)} %param.19) | copy-start | bytes 6291460

commit v4 on v3

--- a/solution.py
+++ b/solution.py
@@ -594,18 +594,20 @@
 
     @pl.when(j == pl.num_programs(1) - 1)
     def _():
-        out_ref[0] = (acc[...] / denom[...]).astype(out_ref.dtype)
-
-
-def attend(lengths, queries, new_kv, cache_kv):
+        result = (acc[...] / denom[...]).astype(out_ref.dtype)
+        out_ref[:, 0] = result.reshape(out_ref.shape[0], out_ref.shape[2], out_ref.shape[3])
+
+
+def attend(lengths, queries, new_kv, cache_kv, parts):
     seq_count, length, width = cache_kv.shape
-    tile = length // 4
+    tile = length // 2
+    heads = H // parts
     return pl.pallas_call(
         functools.partial(_attend_kernel, tile),
-        out_shape=jax.ShapeDtypeStruct((seq_count, H, KV_RANK), queries.dtype),
+        out_shape=jax.ShapeDtypeStruct((parts, seq_count, heads, KV_RANK), queries.dtype),
         grid_spec=pltpu.PrefetchScalarGridSpec(
             num_scalar_prefetch=1,
-            grid=(seq_count, 4),
+            grid=(seq_count, 2),
             in_specs=[
                 pl.BlockSpec((1, H, width), lambda b, j, n: (b, 0, 0)),
                 pl.BlockSpec((1, 1, width), lambda b, j, n: (b, 0, 0)),
@@ -614,7 +616,7 @@
                     lambda b, j, n: (b, 0, jnp.minimum(j, lax.div(n[b] - 1, tile))),
                 ),
             ],
-            out_specs=pl.BlockSpec((1, H, KV_RANK), lambda b, j, n: (b, 0, 0)),
+            out_specs=pl.BlockSpec((parts, 1, heads, KV_RANK), lambda b, j, n: (0, b, 0, 0)),
             scratch_shapes=[
                 pltpu.VMEM((H, 1), jnp.float32),
                 pltpu.VMEM((H, 1), jnp.float32),
@@ -678,9 +680,11 @@
     queries = jnp.concatenate(
         [q_lat[i] for i in range(rep_count)] + [q_rope.reshape(seq_count, H, ROPE)], axis=2
     )
-    latent = attend(lengths, queries, new_kv, cache_kv)
-
-    by_heads = latent.reshape(seq_count, group, heads_here, KV_RANK).transpose(1, 0, 2, 3)
+    if heads_here % 8 == 0:
+        by_heads = attend(lengths, queries, new_kv, cache_kv, group)
+    else:
+        latent = attend(lengths, queries, new_kv, cache_kv, 1)
+        by_heads = latent.reshape(seq_count, group, heads_here, KV_RANK).transpose(1, 0, 2, 3)
     latent_here = exchange(
         by_heads.reshape(group, seq_count * heads_here, KV_RANK), "grp", group, False, 3
     ).reshape(group * seq_count, heads_here, KV_RANK)

time: 135 us -> 131 us (0.970)
  local copies, waits for them, and re-layouts: 14.3 us -> 12 us
  Pallas kernels: 114 us -> 112 us
    pallas_call x3, Pallas kernels: 28.5 us -> 25.6 us  [exchange(): pl.pallas_call(functools.partial(_exchange_kernel, axis, n, gather), out_...]
    pallas_call x1, Pallas kernels: 58.4 us -> 60.6 us  [mlp_all(): pl.pallas_call(functools.partial(_mlp_kernel, zs), out_shape=jax.ShapeDty...]
    reshape x1 -> x0, local copies, waits for them, and re-layouts: 1.68 us -> none  [on_device(): by_heads.reshape(group, seq_count * heads_here, KV_RANK)]
  transfers between devices with their start and end apart: 3 -> 3, of which waited for: 0 -> 0; matrix products, arithmetic and copies ran while one was open for 3% -> 2% of each run, Pallas kernels for 23% -> 21%
where the time goes in v4:
time: 131 us; the launch traced here: 130 us
  Pallas kernels  112 us (85%)
  local copies, waits for them, and re-layouts  12 us (9%)
  starting transfers between devices  3.14 us (2%)
  matrix products  2.49 us (2%)
    pallas_call x1, Pallas kernels, mlp_all(): pl.pallas_call(functools.partial(_mlp_kernel, zs), out_shape=jax.ShapeDty...  60.6 us
    pallas_call x3, Pallas kernels, exchange(): pl.pallas_call(functools.partial(_exchange_kernel, axis, n, gather), out_...  25.6 us
    pallas_call x1, Pallas kernels, attend(): pl.pallas_call(functools.partial(_attend_kernel, tile), out_shape=jax.Sha...  16.2 us
    pallas_call x1, Pallas kernels, half_product(): pl.pallas_call(_half_product_kernel, out_shape=jax.ShapeDtypeStruct((rows...  7.01 us
    ppermute x3, starting transfers between devices, on_device(): lax.ppermute(uv_own, 'rep', [(i, (i + step) % rep_count) for i in range(r...  3.14 us
    pallas_call x1, Pallas kernels, pair_gather(): pl.pallas_call(_pair_kernel, out_shape=[jax.ShapeDtypeStruct((2,) + v.sha...  2.94 us
  transfers between devices with their start and end apart: 3, of which 0 were waited for; matrix products, arithmetic and copies ran while one was open for 2% of the time, Pallas kernels for 21%

profile of v4, /device:TPU:0, one launch (start us, length us, event | category | flops | bytes accessed | tf_op | source)
XLA Modules:
  0.0 130.3 jit_solution(16945959193174729787)
XLA Ops:
  0.0 0.0 copy-start
  0.0 1.7 %reshape.53.x_ref = bf16[256,128]{1,0:T(8,128)(2,1)} reshape(bf16[4,8192]{1,0:T(4,128)(2,1)} %param.14) | data formatting | bytes 131072 | tf_op jit(solution)/shard_map/reshape | solution.py:657
  1.7 7.9 %shard_map.127 = bf16[4,256,128]{2,1,0:T(8,128)(2,1)} custom-call(bf16[256,128]{1,0:T(8,128)(2,1)} %reshape.53.x_ref), custom_call_target="tpu_custom_call" | custom-call | tf_op jit(solution)/shard_map/pallas_call | solution.py:69
  9.6 0.0 copy-done
  9.6 0.0 copy-start.4
  9.6 2.1 %fusion.6 = bf16[16,64,128]{2,0,1:T(8,128)(2,1)S(1)} fusion(bf16[16,64,128]{2,1,0:T(8,128)(2,1)} %bitcast.56, bf16[128,8192]{1,0:T(8,128)(2,1)S(1)} %copy-done), kind=kOutput, calls=%fused_computation.4 | convolution fusion | flops 33685504 | bytes 2621440 | tf_op jit(solution)/shard_map/bhd,chd->bhc/dot_general | solution.py:658
  11.8 0.8 copy.22
  12.6 0.0 copy-start.5
  12.6 7.0 %shard_map.128 = bf16[4,256,128]{2,1,0:T(8,128)(2,1)} custom-call(bf16[4,256,128]{2,1,0:T(8,128)(2,1)} %bitcast.54), custom_call_target="tpu_custom_call" | custom-call | tf_op jit(solution)/shard_map/pallas_call | solution.py:69
  19.6 1.0 constant_dynamic-slice_fusion.2
  20.5 0.7 collective-permute-start
  21.2 1.6 %collective-permute-start.1 = (bf16[128,1024]{1,0:T(8,128)(2,1)S(1)}, bf16[128,1024]{1,0:T(8,128)(2,1)S(1)}, u32[]{:S(2)}, u32[]{:S(2)}) collective-permute-start(bf16[128,1024]{1,0:T(8,128)(2,1)S(1)} %constant_dynamic-slice_fusion.2), channel_id=1, source_target_pairs={{0,16},{8,24},{16,0},{24,8},{1,17},{9,25},{17,1},{25,9},{2,18},{10... | collective-permute-start | bytes 786440 | tf_op jit(solution)/shard_map/ppermute | solution.py:672
  22.9 0.8 collective-permute-start.2
  23.7 1.0 fusion.13
  24.7 0.0 copy-done.4
  24.7 0.1 reshape.57
  24.8 0.1 broadcast_in_dim.20
  25.1 0.0 copy-start.2
  25.1 0.0 copy-done.5
  25.1 0.7 copy.23.new_ref
  25.7 0.1 copy-done.2
  25.8 0.0 copy-start.6
  25.8 16.2 %shard_map.129 = bf16[8,4,8,512]{3,2,1,0:T(8,128)(2,1)} custom-call(s32[4]{0:T(128)} %lengths.1, bf16[4,64,576]{2,1,0:T(8,128)(2,1)} %copy-done.2, bf16[4,1,576]{2,1,0:T(2,128)(2,1)} %copy.23.new_ref, bf16[4,576,4096]{2,1,0:T(8,128)(2,1)} %bitcast.47), custom_call_target="tpu_custom_call" | custom-call | flops 2415919104 | bytes 18874368 | tf_op jit(solution)/shard_map/pallas_call | solution.py:605
  42.0 10.7 %shard_map.130 = bf16[8,32,512]{2,1,0:T(8,128)(2,1)} custom-call(bf16[8,32,512]{2,1,0:T(8,128)(2,1)} %bitcast.52), custom_call_target="tpu_custom_call" | custom-call | tf_op jit(solution)/shard_map/pallas_call | solution.py:69
  52.7 0.0 copy-start.3
  52.7 0.0 copy-done.6
  52.7 0.1 dynamic-slice.3
  52.8 0.6 dynamic_slice.14.gain
  53.4 0.0 collective-permute-done
  53.5 0.0 collective-permute-done.1
  53.5 0.0 collective-permute-done.2
  53.6 0.3 copy.30
  53.8 0.0 copy-done.3
  53.8 0.4 fusion.9
  54.2 0.6 copy.48
  54.8 2.9 %shard_map.131 = (bf16[2,32,1024]{2,1,0:T(8,128)(2,1)}, bf16[2,4,7168]{2,1,0:T(4,128)(2,1)}) custom-call(bf16[32,1024]{1,0:T(8,128)(2,1)} %bitcast.58, bf16[4,7168]{1,0:T(4,128)(2,1)} %r_ref.1), custom_call_target="tpu_custom_call" | custom-call | tf_op jit(solution)/shard_map/pallas_call | solution.py:117
  57.8 1.0 reshape.62
  58.8 0.7 reshape.63.x_ref
  59.5 0.9 reshape.65
  60.4 0.6 constant_dynamic-slice_fusion.1.hid
  61.1 7.0 %shard_map.132 = bf16[64,3584]{1,0:T(8,128)(2,1)} custom-call(s32[1]{0:T(128)} %bitcast.core_ref, bf16[64,1024]{1,0:T(8,128)(2,1)} %reshape.63.x_ref, bf16[1024,7168]{1,0:T(8,128)(2,1)} %w_ref.1), custom_call_target="tpu_custom_call" | custom-call | tf_op jit(solution)/shard_map/pallas_call | solution.py:137
  68.1 0.0 copy-start.1
  68.1 60.6 %shard_map.133 = bf16[8,7168]{1,0:T(8,128)(2,1)} custom-call(bf16[8,8,3584]{2,1,0:T(8,128)(2,1)} %bitcast.51, bf16[8,3584]{1,0:T(8,128)(2,1)} %constant_dynamic-slice_fusion.1.hid, bf16[1,3584]{1,0:T(2,128)(2,1)} %dynamic_slice.14.gain, bf16[576,7168]{1,0:T(8,128)(2,1)} %bitcast.48, bf16[576,7168]{1,0:T(8,128)(2,1)} %bitcast.49, bf16[576,7168]{1,0:T(8,128)(2,1)} %wd_hbm.1), custom_call_target="tpu_custom_call" | custom-call | tf_op jit(solution)/shard_map/pallas_call | solution.py:527
  128.7 1.6 %constant_dynamic-slice_fusion = bf16[4,7168]{1,0:T(4,128)(2,1)} fusion(bf16[8,7168]{1,0:T(8,128)(2,1)} %shard_map.133, s32[]{:T(128)S(6)} %select_n.28), kind=kLoop, calls=%fused_computation.21 | loop fusion | bytes 114692 | tf_op jit(solution)/shard_map/dynamic_slice | solution.py:710
  130.3 0.0 copy-done.1
  (10 shorter events, 0.2 us)
Async XLA Ops:
  0.0 9.6 %copy-start = (bf16[128,8192]{1,0:T(8,128)(2,1)S(1)}, bf16[128,8192]{1,0:T(8,128)(2,1)}, u32[]{:S(2)}) copy-start(bf16[128,8192]{1,0:T(8,128)(2,1)} %param.19) | copy-start | bytes 6291460
  9.6 15.0 %copy-start.4 = (bf16[4,4096]{1,0:T(4,128)(2,1)S(1)}, bf16[4,4096]{1,0:T(4,128)(2,1)}, u32[]{:S(2)}) copy-start(bf16[4,4096]{1,0:T(4,128)(2,1)} %param.15) | copy-start | bytes 98308
  12.6 12.5 %copy-start.5 = (bf16[4,576]{1,0:T(4,128)(2,1)S(1)}, bf16[4,576]{1,0:T(4,128)(2,1)}, u32[]{:S(2)}) copy-start(bf16[4,576]{1,0:T(4,128)(2,1)} %param.16) | copy-start | bytes 13828
  20.5 32.9 %collective-permute-start = (bf16[128,1024]{1,0:T(8,128)(2,1)S(1)}, bf16[128,1024]{1,0:T(8,128)(2,1)S(1)}, u32[]{:S(2)}, u32[]{:S(2)}) collective-permute-start(bf16[128,1024]{1,0:T(8,128)(2,1)S(1)} %constant_dynamic-slice_fusion.2), channel_id=1, source_target_pairs={{0,8},{8,16},{16,24},{24,0},{1,9},{9,17},{17,25},{25,1},{2,10},{10... | collective-permute-start | bytes 786440 | tf_op jit(solution)/shard_map/ppermute | solution.py:672
  21.2 32.2 %collective-permute-start.1 = (bf16[128,1024]{1,0:T(8,128)(2,1)S(1)}, bf16[128,1024]{1,0:T(8,128)(2,1)S(1)}, u32[]{:S(2)}, u32[]{:S(2)}) collective-permute-start(bf16[128,1024]{1,0:T(8,128)(2,1)S(1)} %constant_dynamic-slice_fusion.2), channel_id=1, source_target_pairs={{0,16},{8,24},{16,0},{24,8},{1,17},{9,25},{17,1},{25,9},{2,18},{10... | collective-permute-start | bytes 786440 | tf_op jit(solution)/shard_map/ppermute | solution.py:672
  22.9 30.6 %collective-permute-start.2 = (bf16[128,1024]{1,0:T(8,128)(2,1)S(1)}, bf16[128,1024]{1,0:T(8,128)(2,1)S(1)}, u32[]{:S(2)}, u32[]{:S(2)}) collective-permute-start(bf16[128,1024]{1,0:T(8,128)(2,1)S(1)} %constant_dynamic-slice_fusion.2), channel_id=1, source_target_pairs={{0,24},{8,0},{16,8},{24,16},{1,25},{9,1},{17,9},{25,17},{2,26},{10... | collective-permute-start | bytes 786440 | tf_op jit(solution)/shard_map/ppermute | solution.py:672
  25.1 0.7 copy-start.2
  25.8 26.9 %copy-start.6 = (bf16[7168]{0:T(1024)(128)(2,1)S(1)}, bf16[7168]{0:T(1024)(128)(2,1)}, u32[]{:S(2)}) copy-start(bf16[7168]{0:T(1024)(128)(2,1)} %param.22) | copy-start | bytes 43012
  52.7 1.1 copy-start.3
  68.1 62.2 %copy-start.1 = (bf16[128,8192]{1,0:T(8,128)(2,1)S(1)}, bf16[128,8192]{1,0:T(8,128)(2,1)}, u32[]{:S(2)}) copy-start(bf16[128,8192]{1,0:T(8,128)(2,1)} %param.19) | copy-start | bytes 6291460
